TPU v7x, 8 devices: a whole 2x2x1 slice. The times are simulated.
8 devices in a mesh: dp: 1 (over z), pp: 8 (over y, x, core).
Axes of the slice: x: 2, y: 2, z: 1, core: 2. Of those that a mesh axis runs over, the one named last changes fastest.
Arguments:
- x_in: bfloat16 [8, 1, 128, 1024], P(('dp', 'pp'))
- dy_out: bfloat16 [8, 1, 128, 1024], P(('dp', 'pp'))
- w_qkv: bfloat16 [8, 2, 1, 1024, 3, 16, 64], P('pp')
- w_attn: bfloat16 [8, 2, 1, 16, 64, 1024], P('pp')
- w_fc: bfloat16 [8, 2, 1, 1024, 4096], P('pp')
- w_proj: bfloat16 [8, 2, 1, 4096, 1024], P('pp')
- b_qkv: bfloat16 [8, 2, 1, 3, 16, 64], P('pp')
- b_fc: bfloat16 [8, 2, 1, 4096], P('pp')
- vec_d: bfloat16 [8, 2, 1, 6, 1024], P('pp')
Outputs:
- output 1: bfloat16 [8, 1, 128, 1024], P(('dp', 'pp'))
- output 2: bfloat16 [8, 1, 128, 1024], P(('dp', 'pp'))
- output 3: float32 [8, 2, 1, 1024, 3, 16, 64], P(('dp', 'pp'))
- output 4: float32 [8, 2, 1, 16, 64, 1024], P(('dp', 'pp'))
- output 5: float32 [8, 2, 1, 1024, 4096], P(('dp', 'pp'))
- output 6: float32 [8, 2, 1, 4096, 1024], P(('dp', 'pp'))
- output 7: float32 [8, 2, 1, 3, 16, 64], P(('dp', 'pp'))
- output 8: float32 [8, 2, 1, 4096], P(('dp', 'pp'))
- output 9: float32 [8, 2, 1, 6, 1024], P(('dp', 'pp'))
All inputs are finite; a program needn't handle non-finite values.
Results may differ from a plain program's by a relative error of at most 0.02.
Values are sent between devices in bfloat16 or wider.
A program may use at most 1 GiB of HBM per device.

v0:
```python
import jax
import jax.numpy as jnp
from jax import lax
from jax.sharding import PartitionSpec as P

EPSILON = 1e-5


def layer_norm(rows_in, ln_gain, ln_shift):
    rows_f32 = rows_in.astype(jnp.float32)
    row_mean = jnp.mean(rows_f32, axis=-1, keepdims=True)
    centered = rows_f32 - row_mean
    row_var = jnp.mean(centered * centered, axis=-1, keepdims=True)
    scaled = centered * lax.rsqrt(row_var + EPSILON)
    return (scaled * ln_gain.astype(jnp.float32) + ln_shift.astype(jnp.float32)).astype(jnp.bfloat16)


def gpt_layer(hidden_in, layer_w):
    w_qkv, w_attn, w_fc, w_proj, b_qkv, b_fc, vec_d = layer_w
    n_batch, seq_len, d_model = hidden_in.shape
    n_heads, head_dim = w_qkv.shape[-2], w_qkv.shape[-1]
    tokens = n_batch * seq_len
    flat_rows = hidden_in.reshape(tokens, d_model)
    normed = layer_norm(flat_rows, vec_d[0], vec_d[1])
    qkv_proj = jnp.dot(normed, w_qkv.reshape(d_model, 3 * d_model), preferred_element_type=jnp.float32)
    qkv_proj = (qkv_proj + b_qkv.reshape(3 * d_model).astype(jnp.float32)).astype(jnp.bfloat16)
    qkv_proj = qkv_proj.reshape(n_batch, seq_len, 3, n_heads, head_dim)
    query_heads = qkv_proj[:, :, 0]
    key_heads = qkv_proj[:, :, 1]
    value_heads = qkv_proj[:, :, 2]
    scores = jnp.einsum('bqhe,bkhe->bhqk', query_heads, key_heads, preferred_element_type=jnp.float32) * (head_dim ** -0.5)
    causal = lax.broadcasted_iota(jnp.int32, (seq_len, seq_len), 0) >= lax.broadcasted_iota(jnp.int32, (seq_len, seq_len), 1)
    scores = jnp.where(causal, scores, -1e30)
    attn_probs = jax.nn.softmax(scores, axis=-1).astype(jnp.bfloat16)
    mixed_heads = jnp.einsum('bhqk,bkhe->bqhe', attn_probs, value_heads, preferred_element_type=jnp.float32).astype(jnp.bfloat16)
    attn_out = jnp.dot(mixed_heads.reshape(tokens, d_model), w_attn.reshape(d_model, d_model), preferred_element_type=jnp.float32)
    residual = (flat_rows.astype(jnp.float32) + attn_out + vec_d[2].astype(jnp.float32)).astype(jnp.bfloat16)
    normed_two = layer_norm(residual, vec_d[3], vec_d[4])
    hidden = jnp.dot(normed_two, w_fc, preferred_element_type=jnp.float32) + b_fc.astype(jnp.float32)
    hidden = jax.nn.gelu(hidden, approximate=True).astype(jnp.bfloat16)
    mlp_out = jnp.dot(hidden, w_proj, preferred_element_type=jnp.float32) + vec_d[5].astype(jnp.float32)
    return (residual.astype(jnp.float32) + mlp_out).astype(jnp.bfloat16).reshape(n_batch, seq_len, d_model)


def stage_forward(hidden_in, stage_w):
    for layer_idx in range(stage_w[0].shape[0]):
        hidden_in = gpt_layer(hidden_in, tuple(t[layer_idx] for t in stage_w))
    return hidden_in


def skip_forward(hidden_in, stage_w):
    return jnp.zeros_like(hidden_in)


def stage_backward(hidden_in, cotangent, stage_w, grad_acc):
    _, pull_back = jax.vjp(stage_forward, hidden_in, stage_w)
    d_input, d_weights = pull_back(cotangent)
    return d_input, tuple(a + g.astype(jnp.float32) for a, g in zip(grad_acc, d_weights))


def skip_backward(hidden_in, cotangent, stage_w, grad_acc):
    return jnp.zeros_like(hidden_in), grad_acc


def pick_row(buffer, index):
    return lax.dynamic_index_in_dim(buffer, index, 0, keepdims=False)


def store_row(buffer, row_val, index):
    return lax.dynamic_update_index_in_dim(buffer, row_val, index, 0)


def solution(mesh):
    n_stages = mesh.shape['pp']
    last = n_stages - 1
    to_next = [(i, i + 1) for i in range(last)]
    to_prev = [(i + 1, i) for i in range(last)]
    opposite = [(i, last - i) for i in range(n_stages)]
    data_spec = P(('dp', 'pp'))
    weight_spec = P('pp')

    def per_device(x_loc, dy_loc, *weights):
        dev_pos = lax.axis_index('pp')
        down_w = tuple(t[0, 0] for t in weights)
        up_w = tuple(t[0, 1] for t in weights)
        x_all = lax.all_gather(x_loc, 'pp', tiled=True)
        dy_all = lax.all_gather(dy_loc, 'pp', tiled=True)
        n_micro = x_all.shape[0]
        half_micro = n_micro // 2
        n_steps = half_micro + last
        act_shape = x_loc.shape[1:]
        zero_act = jnp.zeros(act_shape, x_loc.dtype)
        stash_zero = jnp.zeros((half_micro + 1,) + act_shape, x_loc.dtype)
        out_zero = jnp.zeros((n_micro + 1,) + act_shape, x_loc.dtype)

        def forward_step(step, carry):
            down_in, up_in, down_stash, up_stash, y_buf = carry
            down_idx = step - dev_pos
            up_idx = step - (last - dev_pos)
            down_ok = (down_idx >= 0) & (down_idx < half_micro)
            up_ok = (up_idx >= 0) & (up_idx < half_micro)
            down_row = jnp.clip(down_idx, 0, half_micro - 1)
            up_row = jnp.clip(up_idx, 0, half_micro - 1)
            down_act = jnp.where(dev_pos == 0, pick_row(x_all, down_row), down_in)
            up_act = jnp.where(dev_pos == last, pick_row(x_all, half_micro + up_row), up_in)
            down_stash = store_row(down_stash, down_act, jnp.where(down_ok, down_idx, half_micro))
            up_stash = store_row(up_stash, up_act, jnp.where(up_ok, up_idx, half_micro))
            down_out = lax.cond(down_ok, stage_forward, skip_forward, down_act, down_w)
            up_out = lax.cond(up_ok, stage_forward, skip_forward, up_act, up_w)
            y_buf = store_row(y_buf, down_out, jnp.where(down_ok & (dev_pos == last), down_idx, n_micro))
            y_buf = store_row(y_buf, up_out, jnp.where(up_ok & (dev_pos == 0), half_micro + up_idx, n_micro))
            down_in = lax.ppermute(down_out, 'pp', to_next)
            up_in = lax.ppermute(up_out, 'pp', to_prev)
            return down_in, up_in, down_stash, up_stash, y_buf

        fwd_init = (zero_act, zero_act, stash_zero, stash_zero, out_zero)
        _, _, down_stash, up_stash, y_buf = lax.fori_loop(0, n_steps, forward_step, fwd_init)
        y_loc = lax.psum_scatter(y_buf[:n_micro], 'pp', scatter_dimension=0, tiled=True)
        grad_zero = tuple(jnp.zeros(t.shape, jnp.float32) for t in down_w)

        def backward_step(step, carry):
            down_cot_in, up_cot_in, down_acc, up_acc, dx_buf = carry
            down_idx = step - (last - dev_pos)
            up_idx = step - dev_pos
            down_ok = (down_idx >= 0) & (down_idx < half_micro)
            up_ok = (up_idx >= 0) & (up_idx < half_micro)
            down_row = jnp.clip(down_idx, 0, half_micro - 1)
            up_row = jnp.clip(up_idx, 0, half_micro - 1)
            down_cot = jnp.where(dev_pos == last, pick_row(dy_all, down_row), down_cot_in)
            up_cot = jnp.where(dev_pos == 0, pick_row(dy_all, half_micro + up_row), up_cot_in)
            down_dx, down_acc = lax.cond(down_ok, stage_backward, skip_backward, pick_row(down_stash, down_row), down_cot, down_w, down_acc)
            up_dx, up_acc = lax.cond(up_ok, stage_backward, skip_backward, pick_row(up_stash, up_row), up_cot, up_w, up_acc)
            dx_buf = store_row(dx_buf, down_dx, jnp.where(down_ok & (dev_pos == 0), down_idx, n_micro))
            dx_buf = store_row(dx_buf, up_dx, jnp.where(up_ok & (dev_pos == last), half_micro + up_idx, n_micro))
            down_cot_in = lax.ppermute(down_dx, 'pp', to_prev)
            up_cot_in = lax.ppermute(up_dx, 'pp', to_next)
            return down_cot_in, up_cot_in, down_acc, up_acc, dx_buf

        bwd_init = (zero_act, zero_act, grad_zero, grad_zero, out_zero)
        _, _, down_acc, up_acc, dx_buf = lax.fori_loop(0, n_steps, backward_step, bwd_init)
        dx_loc = lax.psum_scatter(dx_buf[:n_micro], 'pp', scatter_dimension=0, tiled=True)
        peer_down = tuple(lax.ppermute(g, 'pp', opposite) for g in down_acc)
        peer_up = tuple(lax.ppermute(g, 'pp', opposite) for g in up_acc)
        grads = tuple(jnp.stack([mine_d + peer_u, mine_u + peer_d], axis=0)[None] for mine_d, mine_u, peer_d, peer_u in zip(down_acc, up_acc, peer_down, peer_up))
        return (y_loc, dx_loc) + grads

    return jax.shard_map(per_device, mesh=mesh, in_specs=(data_spec, data_spec) + (weight_spec,) * 7, out_specs=(data_spec, data_spec) + (data_spec,) * 7, check_vma=False)
```

profile of v0, /device:TPU:0, one launch (start us, length us, event | category | flops | bytes accessed | tf_op | source)
XLA Modules:
  0.0 4906.5 jit_solution(7833738573962327782)
XLA Ops:
  50.5 533.5 %while.70 = (s32[]{:T(128)}, bf16[1,128,1024]{2,1,0:T(8,128)(2,1)}, bf16[1,128,1024]{2,1,0:T(8,128)(2,1)S(1)}, bf16[5,1,128,1024]{3,2,1,0:T(8,128)(2,1)}, bf16[5...) while((s32[]{:T(128)}, bf16[1,128,1024]{2,1,0:T(8,128)(2,1)}, ...), condition=%wide.region_17.18_spmd, body=%wide.region_0.17_spmd.sunk | while | flops 6668739584 | bytes 84828144 | solution.py:117
  205.1 32.1 collective-permute-start
  255.0 46.5 collective-permute-done.1
  304.4 37.3 collective-permute-start
  373.4 34.5 collective-permute-start
  641.1 1863.3 %while.71 = (s32[]{:T(128)}, bf16[1,128,1024]{2,1,0:T(8,128)(2,1)}, bf16[1,128,1024]{2,1,0:T(8,128)(2,1)}, f32[1,1024,3,16,64]{1,4,3,2,0:T(8,128)}, f32[1,16,64,...) while((s32[]{:T(128)}, bf16[1,128,1024]{2,1,0:T(8,128)(2,1)}, ...), condition=%wide.region_62.63_spmd, body=%wide.region_19.62_spmd.sunk | while | flops 17728512000 | bytes 946527872 | solution.py:140
  659.8 125.9 %conditional.11 = (bf16[1,128,1024]{2,1,0:T(8,128)(2,1)}, f32[1,1024,3,16,64]{1,4,3,2,0:T(8,128)}, f32[1,16,64,1024]{3,2,1,0:T(8,128)}, f32[1,1024,4096]{2,1,0:T...) conditional(s32[]{:T(128)} %convert_element_type.1755, ...), branch_computations={%region_41.41_spmd, %region_42.61_spmd} | conditional | flops 8864256000 | bytes 457747968 | solution.py:132
  809.7 116.7 %conditional.11 = (bf16[1,128,1024]{2,1,0:T(8,128)(2,1)}, f32[1,1024,3,16,64]{1,4,3,2,0:T(8,128)}, f32[1,16,64,1024]{3,2,1,0:T(8,128)}, f32[1,1024,4096]{2,1,0:T...) conditional(s32[]{:T(128)} %convert_element_type.1755, ...), branch_computations={%region_41.41_spmd, %region_42.61_spmd} | conditional | flops 8864256000 | bytes 457747968 | solution.py:132
  952.2 125.9 %conditional.11 = (bf16[1,128,1024]{2,1,0:T(8,128)(2,1)}, f32[1,1024,3,16,64]{1,4,3,2,0:T(8,128)}, f32[1,16,64,1024]{3,2,1,0:T(8,128)}, f32[1,1024,4096]{2,1,0:T...) conditional(s32[]{:T(128)} %convert_element_type.1755, ...), branch_computations={%region_41.41_spmd, %region_42.61_spmd} | conditional | flops 8864256000 | bytes 457747968 | solution.py:132
  1103.9 116.7 %conditional.11 = (bf16[1,128,1024]{2,1,0:T(8,128)(2,1)}, f32[1,1024,3,16,64]{1,4,3,2,0:T(8,128)}, f32[1,16,64,1024]{3,2,1,0:T(8,128)}, f32[1,1024,4096]{2,1,0:T...) conditional(s32[]{:T(128)} %convert_element_type.1755, ...), branch_computations={%region_41.41_spmd, %region_42.61_spmd} | conditional | flops 8864256000 | bytes 457747968 | solution.py:132
  1250.4 128.3 %collective-permute-start.3 = (bf16[1,128,1024]{2,1,0:T(8,128)(2,1)}, bf16[1,128,1024]{2,1,0:T(8,128)(2,1)S(1)}, u32[]{:S(2)}, u32[]{:S(2)}) collective-permute-start(bf16[1,128,1024]{2,1,0:T(8,128)(2,1)} %get-tuple-element.2630), channel_id=1, source_target_pairs={{0,1},{1,2},{2,3},{3,4},{4,5},{5,6},{6,7}} | collective-permute-start | bytes 786440 | tf_op jit(solution)/shard_map/while/body/eval_jaxpr/ppermute | solution.py:136
  1387.3 29.0 collective-permute-start.3
  1424.6 424.3 %collective-permute-start.3 = (bf16[1,128,1024]{2,1,0:T(8,128)(2,1)}, bf16[1,128,1024]{2,1,0:T(8,128)(2,1)S(1)}, u32[]{:S(2)}, u32[]{:S(2)}) collective-permute-start(bf16[1,128,1024]{2,1,0:T(8,128)(2,1)} %get-tuple-element.2630), channel_id=1, source_target_pairs={{0,1},{1,2},{2,3},{3,4},{4,5},{5,6},{6,7}} | collective-permute-start | bytes 786440 | tf_op jit(solution)/shard_map/while/body/eval_jaxpr/ppermute | solution.py:136
  1853.0 115.0 %conditional.10 = (bf16[1,128,1024]{2,1,0:T(8,128)(2,1)}, f32[1,1024,3,16,64]{1,4,3,2,0:T(8,128)}, f32[1,16,64,1024]{3,2,1,0:T(8,128)}, f32[1,1024,4096]{2,1,0:T...) conditional(s32[]{:T(128)} %convert_element_type.1754, ...), branch_computations={%region_20.20_spmd, %region_21.40_spmd} | conditional | flops 8864256000 | bytes 484584736 | solution.py:131
  1987.6 114.9 %conditional.10 = (bf16[1,128,1024]{2,1,0:T(8,128)(2,1)}, f32[1,1024,3,16,64]{1,4,3,2,0:T(8,128)}, f32[1,16,64,1024]{3,2,1,0:T(8,128)}, f32[1,1024,4096]{2,1,0:T...) conditional(s32[]{:T(128)} %convert_element_type.1754, ...), branch_computations={%region_20.20_spmd, %region_21.40_spmd} | conditional | flops 8864256000 | bytes 484584736 | solution.py:131
  2113.0 113.3 %collective-permute-start.3 = (bf16[1,128,1024]{2,1,0:T(8,128)(2,1)}, bf16[1,128,1024]{2,1,0:T(8,128)(2,1)S(1)}, u32[]{:S(2)}, u32[]{:S(2)}) collective-permute-start(bf16[1,128,1024]{2,1,0:T(8,128)(2,1)} %get-tuple-element.2630), channel_id=1, source_target_pairs={{0,1},{1,2},{2,3},{3,4},{4,5},{5,6},{6,7}} | collective-permute-start | bytes 786440 | tf_op jit(solution)/shard_map/while/body/eval_jaxpr/ppermute | solution.py:136
  2230.5 114.8 %conditional.10 = (bf16[1,128,1024]{2,1,0:T(8,128)(2,1)}, f32[1,1024,3,16,64]{1,4,3,2,0:T(8,128)}, f32[1,16,64,1024]{3,2,1,0:T(8,128)}, f32[1,1024,4096]{2,1,0:T...) conditional(s32[]{:T(128)} %convert_element_type.1754, ...), branch_computations={%region_20.20_spmd, %region_21.40_spmd} | conditional | flops 8864256000 | bytes 484584736 | solution.py:131
  2366.2 114.8 %conditional.10 = (bf16[1,128,1024]{2,1,0:T(8,128)(2,1)}, f32[1,1024,3,16,64]{1,4,3,2,0:T(8,128)}, f32[1,16,64,1024]{3,2,1,0:T(8,128)}, f32[1,1024,4096]{2,1,0:T...) conditional(s32[]{:T(128)} %convert_element_type.1754, ...), branch_computations={%region_20.20_spmd, %region_21.40_spmd} | conditional | flops 8864256000 | bytes 484584736 | solution.py:131
  2504.4 158.4 %collective-permute-start.5 = (f32[1,1024,3,16,64]{1,4,3,2,0:T(8,128)}, f32[1,1024,3,16,64]{1,4,3,2,0:T(8,128)}, u32[]{:S(2)}, u32[]{:S(2)}) collective-permute-start(f32[1,1024,3,16,64]{1,4,3,2,0:T(8,128)} %get-tuple-element.1965), channel_id=1, source_target_pairs={{0,7},{1,6},{2,5},{3,4},{4,3},{5,2},{6,1},{7,0}} | collective-permute-start | bytes 37748744 | tf_op jit(solution)/shard_map/ppermute | solution.py:142
  2668.1 804.8 %collective-permute-done.13 = f32[1,3,16,64]{3,2,1,0:T(8,128)S(1)} collective-permute-done((f32[1,3,16,64]{3,2,1,0:T(8,128)}, f32[1,3,16,64]{3,2,1,0:T(8,128)S(1)}, u32[]{:S(2)}, u32[]{:S(2)}) %collective-permute-start.13) | collective-permute-done | bytes 12320 | tf_op jit(solution)/shard_map/ppermute | solution.py:142
  3538.4 237.4 %collective-permute-done.4 = f32[1,1024,3,16,64]{1,4,3,2,0:T(8,128)} collective-permute-done((f32[1,1024,3,16,64]{1,4,3,2,0:T(8,128)}, f32[1,1024,3,16,64]{1,4,3,2,0:T(8,128)}, u32[]{:S(2)}, u32[]{:S(2)}) %collective-permute-start.4) | collective-permute-done | bytes 12582944 | tf_op jit(solution)/shard_map/ppermute | solution.py:143
  3823.1 321.4 %collective-permute-done.8 = f32[1,1024,4096]{2,1,0:T(8,128)} collective-permute-done((f32[1,1024,4096]{2,1,0:T(8,128)}, f32[1,1024,4096]{2,1,0:T(8,128)}, u32[]{:S(2)}, u32[]{:S(2)}) %collective-permute-start.8) | collective-permute-done | bytes 16777248 | tf_op jit(solution)/shard_map/ppermute | solution.py:143
  4182.3 321.7 %collective-permute-done.11 = f32[1,4096,1024]{2,1,0:T(8,128)} collective-permute-done((f32[1,4096,1024]{2,1,0:T(8,128)}, f32[1,4096,1024]{2,1,0:T(8,128)}, u32[]{:S(2)}, u32[]{:S(2)}) %collective-permute-start.11) | collective-permute-done | bytes 16777248 | tf_op jit(solution)/shard_map/ppermute | solution.py:142
  4521.0 342.5 %collective-permute-done.10 = f32[1,4096,1024]{2,1,0:T(8,128)} collective-permute-done((f32[1,4096,1024]{2,1,0:T(8,128)}, f32[1,4096,1024]{2,1,0:T(8,128)}, u32[]{:S(2)}, u32[]{:S(2)}) %collective-permute-start.10) | collective-permute-done | bytes 16777248 | tf_op jit(solution)/shard_map/ppermute | solution.py:143
  (1749 shorter events, 2085.5 us)
Async XLA Ops:
  7.9 576.1 %all-gather.5.cloned.1.call-start = ((), (), s32[]{:S(2)}) async-start(), calls=%async_computation.4 | async-start | bytes 2359296 | tf_op jit(solution)/shard_map/all_gather | solution.py:87
  8.7 4891.0 %reduce-scatter.3.cloned.1.call-start = ((), (), s32[]{:S(2)}) async-start(), calls=%async_computation.3 | async-start | bytes 2359296 | tf_op jit(solution)/shard_map/reduce_scatter | solution.py:118
  251.3 50.2 %collective-permute-start.1 = (bf16[1,128,1024]{2,1,0:T(8,128)(2,1)}, bf16[1,128,1024]{2,1,0:T(8,128)(2,1)S(1)}, u32[]{:S(2)}, u32[]{:S(2)}) collective-permute-start(bf16[1,128,1024]{2,1,0:T(8,128)(2,1)} %get-tuple-element.2585), channel_id=1, source_target_pairs={{1,0},{2,1},{3,2},{4,3},{5,4},{6,5},{7,6}} | collective-permute-start | bytes 786440 | tf_op jit(solution)/shard_map/while/body/eval_jaxpr/ppermute | solution.py:113
  373.4 64.9 %collective-permute-start = (bf16[1,128,1024]{2,1,0:T(8,128)(2,1)}, bf16[1,128,1024]{2,1,0:T(8,128)(2,1)}, u32[]{:S(2)}, u32[]{:S(2)}) collective-permute-start(bf16[1,128,1024]{2,1,0:T(8,128)(2,1)} %get-tuple-element.2583), channel_id=1, source_target_pairs={{0,1},{1,2},{2,3},{3,4},{4,5},{5,6},{6,7}} | collective-permute-start | bytes 786440 | tf_op jit(solution)/shard_map/while/body/eval_jaxpr/ppermute | solution.py:112
  658.4 132.0 %collective-permute-start.2 = (bf16[1,128,1024]{2,1,0:T(8,128)(2,1)}, bf16[1,128,1024]{2,1,0:T(8,128)(2,1)}, u32[]{:S(2)}, u32[]{:S(2)}) collective-permute-start(bf16[1,128,1024]{2,1,0:T(8,128)(2,1)} %get-tuple-element.2629), channel_id=1, source_target_pairs={{1,0},{2,1},{3,2},{4,3},{5,4},{6,5},{7,6}} | collective-permute-start | bytes 786440 | tf_op jit(solution)/shard_map/while/body/eval_jaxpr/ppermute | solution.py:135
  808.4 124.4 %collective-permute-start.2 = (bf16[1,128,1024]{2,1,0:T(8,128)(2,1)}, bf16[1,128,1024]{2,1,0:T(8,128)(2,1)}, u32[]{:S(2)}, u32[]{:S(2)}) collective-permute-start(bf16[1,128,1024]{2,1,0:T(8,128)(2,1)} %get-tuple-element.2629), channel_id=1, source_target_pairs={{1,0},{2,1},{3,2},{4,3},{5,4},{6,5},{7,6}} | collective-permute-start | bytes 786440 | tf_op jit(solution)/shard_map/while/body/eval_jaxpr/ppermute | solution.py:135
  950.9 133.7 %collective-permute-start.2 = (bf16[1,128,1024]{2,1,0:T(8,128)(2,1)}, bf16[1,128,1024]{2,1,0:T(8,128)(2,1)}, u32[]{:S(2)}, u32[]{:S(2)}) collective-permute-start(bf16[1,128,1024]{2,1,0:T(8,128)(2,1)} %get-tuple-element.2629), channel_id=1, source_target_pairs={{1,0},{2,1},{3,2},{4,3},{5,4},{6,5},{7,6}} | collective-permute-start | bytes 786440 | tf_op jit(solution)/shard_map/while/body/eval_jaxpr/ppermute | solution.py:135
  1102.6 125.8 %collective-permute-start.2 = (bf16[1,128,1024]{2,1,0:T(8,128)(2,1)}, bf16[1,128,1024]{2,1,0:T(8,128)(2,1)}, u32[]{:S(2)}, u32[]{:S(2)}) collective-permute-start(bf16[1,128,1024]{2,1,0:T(8,128)(2,1)} %get-tuple-element.2629), channel_id=1, source_target_pairs={{1,0},{2,1},{3,2},{4,3},{5,4},{6,5},{7,6}} | collective-permute-start | bytes 786440 | tf_op jit(solution)/shard_map/while/body/eval_jaxpr/ppermute | solution.py:135
  1246.5 135.6 %collective-permute-start.2 = (bf16[1,128,1024]{2,1,0:T(8,128)(2,1)}, bf16[1,128,1024]{2,1,0:T(8,128)(2,1)}, u32[]{:S(2)}, u32[]{:S(2)}) collective-permute-start(bf16[1,128,1024]{2,1,0:T(8,128)(2,1)} %get-tuple-element.2629), channel_id=1, source_target_pairs={{1,0},{2,1},{3,2},{4,3},{5,4},{6,5},{7,6}} | collective-permute-start | bytes 786440 | tf_op jit(solution)/shard_map/while/body/eval_jaxpr/ppermute | solution.py:135
  1250.4 131.7 %collective-permute-start.3 = (bf16[1,128,1024]{2,1,0:T(8,128)(2,1)}, bf16[1,128,1024]{2,1,0:T(8,128)(2,1)S(1)}, u32[]{:S(2)}, u32[]{:S(2)}) collective-permute-start(bf16[1,128,1024]{2,1,0:T(8,128)(2,1)} %get-tuple-element.2630), channel_id=1, source_target_pairs={{0,1},{1,2},{2,3},{3,4},{4,5},{5,6},{6,7}} | collective-permute-start | bytes 786440 | tf_op jit(solution)/shard_map/while/body/eval_jaxpr/ppermute | solution.py:136
  1421.8 430.5 %collective-permute-start.2 = (bf16[1,128,1024]{2,1,0:T(8,128)(2,1)}, bf16[1,128,1024]{2,1,0:T(8,128)(2,1)}, u32[]{:S(2)}, u32[]{:S(2)}) collective-permute-start(bf16[1,128,1024]{2,1,0:T(8,128)(2,1)} %get-tuple-element.2629), channel_id=1, source_target_pairs={{1,0},{2,1},{3,2},{4,3},{5,4},{6,5},{7,6}} | collective-permute-start | bytes 786440 | tf_op jit(solution)/shard_map/while/body/eval_jaxpr/ppermute | solution.py:135
  1424.6 427.7 %collective-permute-start.3 = (bf16[1,128,1024]{2,1,0:T(8,128)(2,1)}, bf16[1,128,1024]{2,1,0:T(8,128)(2,1)S(1)}, u32[]{:S(2)}, u32[]{:S(2)}) collective-permute-start(bf16[1,128,1024]{2,1,0:T(8,128)(2,1)} %get-tuple-element.2630), channel_id=1, source_target_pairs={{0,1},{1,2},{2,3},{3,4},{4,5},{5,6},{6,7}} | collective-permute-start | bytes 786440 | tf_op jit(solution)/shard_map/while/body/eval_jaxpr/ppermute | solution.py:136
  2102.5 127.2 %collective-permute-start.2 = (bf16[1,128,1024]{2,1,0:T(8,128)(2,1)}, bf16[1,128,1024]{2,1,0:T(8,128)(2,1)}, u32[]{:S(2)}, u32[]{:S(2)}) collective-permute-start(bf16[1,128,1024]{2,1,0:T(8,128)(2,1)} %get-tuple-element.2629), channel_id=1, source_target_pairs={{1,0},{2,1},{3,2},{4,3},{5,4},{6,5},{7,6}} | collective-permute-start | bytes 786440 | tf_op jit(solution)/shard_map/while/body/eval_jaxpr/ppermute | solution.py:135
  2113.0 116.7 %collective-permute-start.3 = (bf16[1,128,1024]{2,1,0:T(8,128)(2,1)}, bf16[1,128,1024]{2,1,0:T(8,128)(2,1)S(1)}, u32[]{:S(2)}, u32[]{:S(2)}) collective-permute-start(bf16[1,128,1024]{2,1,0:T(8,128)(2,1)} %get-tuple-element.2630), channel_id=1, source_target_pairs={{0,1},{1,2},{2,3},{3,4},{4,5},{5,6},{6,7}} | collective-permute-start | bytes 786440 | tf_op jit(solution)/shard_map/while/body/eval_jaxpr/ppermute | solution.py:136
  2504.4 998.8 %collective-permute-start.5 = (f32[1,1024,3,16,64]{1,4,3,2,0:T(8,128)}, f32[1,1024,3,16,64]{1,4,3,2,0:T(8,128)}, u32[]{:S(2)}, u32[]{:S(2)}) collective-permute-start(f32[1,1024,3,16,64]{1,4,3,2,0:T(8,128)} %get-tuple-element.1965), channel_id=1, source_target_pairs={{0,7},{1,6},{2,5},{3,4},{4,3},{5,2},{6,1},{7,0}} | collective-permute-start | bytes 37748744 | tf_op jit(solution)/shard_map/ppermute | solution.py:142
  2662.8 833.8 %collective-permute-start.7 = (f32[1,16,64,1024]{3,2,1,0:T(8,128)}, f32[1,16,64,1024]{3,2,1,0:T(8,128)S(1)}, u32[]{:S(2)}, u32[]{:S(2)}) collective-permute-start(f32[1,16,64,1024]{3,2,1,0:T(8,128)} %get-tuple-element.1967), channel_id=1, source_target_pairs={{0,7},{1,6},{2,5},{3,4},{4,3},{5,2},{6,1},{7,0}} | collective-permute-start | bytes 12582920 | tf_op jit(solution)/shard_map/ppermute | solution.py:142
  2662.8 1142.1 %collective-permute-start.9 = (f32[1,1024,4096]{2,1,0:T(8,128)}, f32[1,1024,4096]{2,1,0:T(8,128)}, u32[]{:S(2)}, u32[]{:S(2)}) collective-permute-start(f32[1,1024,4096]{2,1,0:T(8,128)} %get-tuple-element.1969), channel_id=1, source_target_pairs={{0,7},{1,6},{2,5},{3,4},{4,3},{5,2},{6,1},{7,0}} | collective-permute-start | bytes 50331656 | tf_op jit(solution)/shard_map/ppermute | solution.py:142
  2665.4 831.2 %collective-permute-start.6 = (f32[1,16,64,1024]{3,2,1,0:T(8,128)}, f32[1,16,64,1024]{3,2,1,0:T(8,128)S(1)}, u32[]{:S(2)}, u32[]{:S(2)}) collective-permute-start(f32[1,16,64,1024]{3,2,1,0:T(8,128)} %get-tuple-element.1968), channel_id=1, source_target_pairs={{0,7},{1,6},{2,5},{3,4},{4,3},{5,2},{6,1},{7,0}} | collective-permute-start | bytes 12582920 | tf_op jit(solution)/shard_map/ppermute | solution.py:143
  2665.4 807.4 %collective-permute-start.13 = (f32[1,3,16,64]{3,2,1,0:T(8,128)}, f32[1,3,16,64]{3,2,1,0:T(8,128)S(1)}, u32[]{:S(2)}, u32[]{:S(2)}) collective-permute-start(f32[1,3,16,64]{3,2,1,0:T(8,128)} %get-tuple-element.1973), channel_id=1, source_target_pairs={{0,7},{1,6},{2,5},{3,4},{4,3},{5,2},{6,1},{7,0}} | collective-permute-start | bytes 36872 | tf_op jit(solution)/shard_map/ppermute | solution.py:142
  3494.0 281.9 %collective-permute-start.4 = (f32[1,1024,3,16,64]{1,4,3,2,0:T(8,128)}, f32[1,1024,3,16,64]{1,4,3,2,0:T(8,128)}, u32[]{:S(2)}, u32[]{:S(2)}) collective-permute-start(f32[1,1024,3,16,64]{1,4,3,2,0:T(8,128)} %get-tuple-element.1966), channel_id=1, source_target_pairs={{0,7},{1,6},{2,5},{3,4},{4,3},{5,2},{6,1},{7,0}} | collective-permute-start | bytes 37748744 | tf_op jit(solution)/shard_map/ppermute | solution.py:143
  3496.6 647.9 %collective-permute-start.8 = (f32[1,1024,4096]{2,1,0:T(8,128)}, f32[1,1024,4096]{2,1,0:T(8,128)}, u32[]{:S(2)}, u32[]{:S(2)}) collective-permute-start(f32[1,1024,4096]{2,1,0:T(8,128)} %get-tuple-element.1970), channel_id=1, source_target_pairs={{0,7},{1,6},{2,5},{3,4},{4,3},{5,2},{6,1},{7,0}} | collective-permute-start | bytes 50331656 | tf_op jit(solution)/shard_map/ppermute | solution.py:143
  3496.6 1007.4 %collective-permute-start.11 = (f32[1,4096,1024]{2,1,0:T(8,128)}, f32[1,4096,1024]{2,1,0:T(8,128)}, u32[]{:S(2)}, u32[]{:S(2)}) collective-permute-start(f32[1,4096,1024]{2,1,0:T(8,128)} %get-tuple-element.1971), channel_id=1, source_target_pairs={{0,7},{1,6},{2,5},{3,4},{4,3},{5,2},{6,1},{7,0}} | collective-permute-start | bytes 50331656 | tf_op jit(solution)/shard_map/ppermute | solution.py:142
  3503.2 1396.5 %reduce-scatter.5.cloned.1.call-start = ((), (), s32[]{:S(2)}) async-start(), calls=%async_computation.5 | async-start | bytes 2359296 | tf_op jit(solution)/shard_map/reduce_scatter | solution.py:141
  3503.2 1360.3 %collective-permute-start.10 = (f32[1,4096,1024]{2,1,0:T(8,128)}, f32[1,4096,1024]{2,1,0:T(8,128)}, u32[]{:S(2)}, u32[]{:S(2)}) collective-permute-start(f32[1,4096,1024]{2,1,0:T(8,128)} %get-tuple-element.1972), channel_id=1, source_target_pairs={{0,7},{1,6},{2,5},{3,4},{4,3},{5,2},{6,1},{7,0}} | collective-permute-start | bytes 50331656 | tf_op jit(solution)/shard_map/ppermute | solution.py:143
  (438 other events, 8197.4 us)
Sparse Core Ops, SparseCore 0:
  9.8 24.7 all-gather.2
  36.4 21.9 all-gather.4
  3503.3 183.9 reduce-scatter.2
  3690.9 321.2 reduce-scatter.4
where the time goes:
time: 4920 us; the launch traced here: 4910 us
  waiting for transfers between devices  2130 us (43%)
  starting transfers between devices  1080 us (22%)
  matrix products  688 us (14%)
  other arithmetic  463 us (9%)
  local copies, waits for them, and re-layouts  402 us (8%)
  loops' own time  129 us (3%)
    ppermute x7, waiting for transfers between devices, per_device(): peer_down = tuple((lax.ppermute(g, 'pp', opposite) for g in down_acc))  1130 us
    ppermute x7, waiting for transfers between devices, per_device(): peer_up = tuple((lax.ppermute(g, 'pp', opposite) for g in up_acc))  905 us
    ppermute x11, starting transfers between devices, backward_step(): up_cot_in = lax.ppermute(up_dx, 'pp', to_next)  719 us
    dot_general x24, matrix products, gpt_layer(): jnp.dot(normed_two, w_fc, preferred_element_type=jnp.float32)  184 us
    dot_general x24, matrix products, gpt_layer(): jnp.dot(hidden, w_proj, preferred_element_type=jnp.float32)  177 us
    ppermute x7, starting transfers between devices, per_device(): peer_down = tuple((lax.ppermute(g, 'pp', opposite) for g in down_acc))  171 us
    ppermute x11, starting transfers between devices, forward_step(): down_in = lax.ppermute(down_out, 'pp', to_next)  152 us
    dot_general x32, matrix products, gpt_layer(): jnp.dot(normed, w_qkv.reshape(d_model, 3 * d_model), preferred_element_ty...  150 us
  transfers between devices with their start and end apart: 62, of which 13 were waited for; matrix products, arithmetic and copies ran while one was open for 20% of the time, Pallas kernels for 0%

commit v1 on v0

v1 whole, which is shorter than its diff:
```python
import jax
import jax.numpy as jnp
from jax import lax
from jax.experimental import pallas as pl
from jax.experimental.pallas import tpu as pltpu
from jax.sharding import PartitionSpec as P

EPSILON = 1e-5
SEQ = 128
DM = 1024
FF = 4096
MICRO = 8
OWN = MICRO // 2
PAIR = 2
PAIRS = MICRO // PAIR
ROWS = PAIR * SEQ
HV, DV, OUT, YO = 0, 2 * MICRO, 4 * MICRO, 6 * MICRO
N_SLOTS = 6 * MICRO + OWN
FWD, BWD = 0, 1
N_TASKS = 24
ORDER = (
    (0x56128398a418820, 0xb5250f3ddc6b34b),
    (0x5a927418a418820, 0xb5250f71eed3598),
    (0x619655112340820, 0xb53d2e434f761a7),
    (0x6958458d4248500, 0xb7a9c96a1879dc6),
)
GELU_C = 0.7978845608028654
GELU_CA = GELU_C * 0.044715
NEG = -1e30
MESH = pl.DeviceIdType.MESH
BF = jnp.bfloat16
F32 = jnp.float32


def dot_nn(a, b):
    return lax.dot_general(a, b, (((1,), (0,)), ((), ())), preferred_element_type=F32)


def dot_nt(a, b):
    return lax.dot_general(a, b, (((1,), (1,)), ((), ())), preferred_element_type=F32)


def dot_tn(a, b):
    return lax.dot_general(a, b, (((0,), (0,)), ((), ())), preferred_element_type=F32)


def normalize(rows_f32):
    mean = jnp.mean(rows_f32, axis=-1, keepdims=True)
    centered = rows_f32 - mean
    var = jnp.mean(centered * centered, axis=-1, keepdims=True)
    rstd = lax.rsqrt(var + EPSILON)
    return centered * rstd, rstd


def rounded(v):
    return v.astype(BF).astype(F32)


def block(j):
    return slice(j * DM, (j + 1) * DM)


def chain_kernel(x_hbm, dy_hbm, wq_hbm, wo_hbm, w1_hbm, w2_hbm, bq_in, bf_in, vec_in,
                 y_hbm, dx_hbm, a_hbm, t_hbm, o_hbm, h1_hbm, n2_hbm, z_hbm, u_hbm, p_hbm,
                 dz_hbm, dt_hbm, dh1_hbm, dh2_hbm, gbq_ref, gbf_ref, gvec_ref,
                 bq_ref, bf_ref, vec_ref, wbuf, w1buf, buf, a_v, t_v, o_v, h1_v, n2_v, z_v, u_v, p_v, dt_v, dh1_v, do_v,
                 wsem, w1sem, fsem, bsem, lsem, recv_x, recv_dy, send_x, send_dy,
                 send_f, recv_f, send_b, recv_b, send_y, recv_y, send_dx, recv_dx):
    me = lax.axis_index('pp')
    dp = lax.axis_index('dp')
    side = me // 4
    pos = me + side * (7 - 2 * me)

    def place(q):
        return (dp, q + side * (7 - 2 * q))

    def copy_of(leg):
        return leg + side - 2 * leg * side

    codes = []
    for s in range(N_TASKS):
        row = [jnp.int32((ORDER[q][s // 12] >> (5 * (s % 12))) % 32) for q in range(4)]
        codes.append(jnp.where(pos == 0, row[0], jnp.where(pos == 1, row[1], jnp.where(pos == 2, row[2], row[3]))))

    def code_at(s):
        c = codes[0]
        for k in range(1, N_TASKS):
            c = jnp.where(s == k, codes[k], c)
        return c

    def parts(code):
        return code // 16, (code // 8) % 2, code % 8

    barrier = pltpu.get_barrier_semaphore()
    for k in range(1, 8):
        pl.semaphore_signal(barrier, inc=1, device_id=(dp, lax.rem(me + k, 8)), device_id_type=MESH)
    pl.semaphore_wait(barrier, 7)

    def block_copy(b, leg):
        c = copy_of(leg)
        if b < 3:
            src = wq_hbm.at[c, pl.ds(b * DM, DM), :]
        elif b == 3:
            src = wo_hbm.at[c]
        else:
            src = w2_hbm.at[c, pl.ds((b - 4) * DM, DM), :]
        return pltpu.make_async_copy(src, wbuf.at[b], wsem.at[b])

    def w1_copy(j, leg):
        return pltpu.make_async_copy(w1_hbm.at[copy_of(leg), :, pl.ds(j * DM, DM)], w1buf.at[leg, j], w1sem.at[leg * 4 + j])

    first_leg = parts(codes[0])[1]
    for b in range(4):
        block_copy(b, first_leg).start()
    for j in range(4):
        w1_copy(j, first_leg).start()
        block_copy(4 + j, first_leg).start()
    for j in range(4):
        w1_copy(j, 1 - first_leg).start()

    def spread(src, base, send, recv, root_side):
        root = root_side * 7
        i = me + root_side * (7 - 2 * me)
        dst = buf.at[base + i]

        @pl.when(me == root)
        def _():
            pltpu.make_async_copy(src, dst, recv.at[i]).start()

        @pl.when(me != root)
        def _():
            pltpu.make_async_remote_copy(src_ref=src, dst_ref=dst, send_sem=send.at[root_side], recv_sem=recv.at[i],
                                         device_id=(dp, root), device_id_type=MESH).start()

    for src, base, send, recv in ((x_hbm, HV, send_x, recv_x), (dy_hbm, DV + MICRO, send_dy, recv_dy)):
        @pl.when(side == 0)
        def _():
            spread(src, base, send, recv, 0)
            spread(src, base, send, recv, 1)

        @pl.when(side == 1)
        def _():
            spread(src, base, send, recv, 1)
            spread(src, base, send, recv, 0)

    for c in range(2):
        bf_ref[c] = bf_in[c:c + 1, :].astype(F32)
        for n in range(6):
            vec_ref[c, n:n + 1, :] = vec_in[n, c:c + 1, :].astype(F32)
        for n in range(24):
            pair = bq_in[c, n // 8, 2 * (n % 8):2 * (n % 8) + 2, :].astype(F32)
            bq_ref[c, :, n * SEQ:(n + 1) * SEQ] = jnp.concatenate([pair[:1], pair[1:]], axis=1)
    gbq_ref[...] = jnp.zeros_like(gbq_ref)
    gbf_ref[...] = jnp.zeros_like(gbf_ref)
    gvec_ref[...] = jnp.zeros_like(gvec_ref)

    def upward(kind, leg):
        return leg if kind == BWD else 1 - leg

    def hop(kind, leg, i):
        k = leg * MICRO + i
        q = pos - 1 + 2 * upward(kind, leg)
        if kind == FWD:
            src, dst, send, recv = buf.at[OUT + k], buf.at[HV + k], send_f.at[k], recv_f.at[k]
        else:
            src, dst = buf.at[pl.ds(OUT + k, PAIR)], buf.at[pl.ds(DV + k, PAIR)]
            send, recv = send_b.at[k // PAIR], recv_b.at[k // PAIR]
        return pltpu.make_async_remote_copy(src_ref=src, dst_ref=dst, send_sem=send, recv_sem=recv,
                                            device_id=place(q), device_id_type=MESH)

    def hops_out(kind, leg):
        up = upward(kind, leg)
        return ((up == 1) & (pos < 3)) | ((up == 0) & (pos > 0))

    def hops_in(kind, leg):
        up = upward(kind, leg)
        return ((up == 1) & (pos > 0)) | ((up == 0) & (pos < 3))

    def f_saves(leg, i):
        pairs = ((a_v, a_hbm), (t_v.at[0], t_hbm), (o_v, o_hbm), (h1_v.at[0], h1_hbm), (n2_v, n2_hbm),
                 (z_v.at[0], z_hbm), (u_v.at[0], u_hbm), (p_v.at[0], p_hbm))
        return [pltpu.make_async_copy(v, h.at[leg, i], fsem.at[n]) for n, (v, h) in enumerate(pairs)]

    def b_saves(leg, i):
        pairs = ((u_v, dz_hbm), (dt_v, dt_hbm), (dh1_v, dh1_hbm), (buf.at[pl.ds(DV + leg * MICRO + i, PAIR)], dh2_hbm))
        return [pltpu.make_async_copy(v, h.at[leg, pl.ds(i, PAIR)], bsem.at[n]) for n, (v, h) in enumerate(pairs)]

    def b_loads(leg, i):
        pairs = ((z_hbm, z_v), (h1_hbm, h1_v), (t_hbm, t_v), (p_hbm, p_v))
        return [pltpu.make_async_copy(h.at[leg, pl.ds(i, PAIR)], v, lsem.at[n]) for n, (h, v) in enumerate(pairs)]

    def to_home(slot, i, dst, send, recv, starting):
        src = buf.at[slot]

        @pl.when(i == 0)
        def _():
            if starting:
                pltpu.make_async_copy(src, dst, recv).start()

        @pl.when((i > 0) & (i < OWN))
        def _():
            rc = pltpu.make_async_remote_copy(src_ref=src, dst_ref=dst, send_sem=send.at[i], recv_sem=recv,
                                              device_id=place(i), device_id_type=MESH)
            if starting:
                rc.start()
            else:
                rc.wait_send()

    lane = lax.broadcasted_iota(jnp.int32, (1, SEQ), 1)
    low = jnp.where(lane < 64, 1.0, 0.0).astype(BF)
    high = jnp.where(lane < 64, 0.0, 1.0).astype(BF)
    q_idx = lax.broadcasted_iota(jnp.int32, (2 * SEQ, SEQ), 0) % SEQ
    k_idx = lax.broadcasted_iota(jnp.int32, (2 * SEQ, SEQ), 1)
    causal = q_idx >= k_idx

    def split_heads(v):
        return jnp.concatenate([v * low, v * high], axis=0)

    def side_by_side(v):
        return jnp.concatenate([v[:SEQ], v[SEQ:]], axis=1)

    def heads(ref, r, part):
        return [ref[r, :, part * DM + p * SEQ:part * DM + (p + 1) * SEQ] for p in range(8)]

    def probs(s):
        s = jnp.where(causal, s * 0.125, NEG)
        e = jnp.exp(s - jnp.max(s, axis=-1, keepdims=True))
        return e * (1.0 / jnp.sum(e, axis=-1, keepdims=True))

    def weights_for(leg, next_leg, fresh, moving):
        def need(*blocks):
            @pl.when(fresh)
            def _():
                for b in blocks:
                    block_copy(b, leg).wait()

        def release(*blocks):
            @pl.when(moving)
            def _():
                for b in blocks:
                    block_copy(b, next_leg).start()

        return need, release

    def forward_task(leg, i, before_kind, before_leg, before_i, need, release):
        c = copy_of(leg)
        k = leg * MICRO + i

        @pl.when((leg == 0) & (pos == 0))
        def _():
            pltpu.make_async_copy(x_hbm, buf.at[HV + i], recv_x.at[i]).wait()

        @pl.when(hops_in(FWD, leg))
        def _():
            hop(FWD, leg, i).wait_recv()

        saves = f_saves(leg, i)
        need(0, 1, 2)
        xh, _ = normalize(buf[HV + k].astype(F32))
        a_v[...] = (xh * vec_ref[c, 0:1, :] + vec_ref[c, 1:2, :]).astype(BF)
        for j in range(3):
            t_v[0, :, block(j)] = (dot_nt(a_v[...], wbuf[j]) + bq_ref[c, :, block(j)]).astype(BF)
        saves[0].start()
        saves[1].start()
        release(0, 1, 2)
        qs = [split_heads(q) for q in heads(t_v, 0, 0)]
        ss = [dot_nt(q, kk) for q, kk in zip(qs, heads(t_v, 0, 1))]
        ps = [probs(sc) for sc in ss]
        for n, (p, v) in enumerate(zip(ps, heads(t_v, 0, 2))):
            p_v[0, n] = p
            o_v[:, n * SEQ:(n + 1) * SEQ] = dot_nn(side_by_side(p.astype(BF)), split_heads(v)).astype(BF)
        saves[2].start()
        saves[7].start()
        need(3)
        h1 = (buf[HV + k].astype(F32) + dot_nn(o_v[...], wbuf[3]) + vec_ref[c, 2:3, :]).astype(BF)
        h1_v[0] = h1
        xh, _ = normalize(h1_v[0].astype(F32))
        n2_v[...] = (xh * vec_ref[c, 3:4, :] + vec_ref[c, 4:5, :]).astype(BF)
        saves[3].start()
        saves[4].start()
        release(3)
        need(4, 5, 6, 7)

        @pl.when(i == 0)
        def _():
            for j in range(4):
                w1_copy(j, leg).wait()

        @pl.when(before_kind == FWD)
        def _():
            for sv in f_saves(before_leg, before_i)[5:7]:
                sv.wait()

        def hidden(j):
            z = dot_nn(n2_v[...], w1buf[leg, j]) + bf_ref[c, :, block(j)]
            zz = z * z
            th = jnp.tanh(z * (GELU_C + GELU_CA * zz))
            half = 0.5 + 0.5 * th
            u_v[0, :, block(j)] = (z * half).astype(BF)
            z_v[0, :, block(j)] = half + ((half * (1.0 - th)) * z) * (GELU_C + (3.0 * GELU_CA) * zz)

        hidden(0)
        acc = jnp.zeros((SEQ, DM), F32)
        for j in range(4):
            if j < 3:
                hidden(j + 1)
            acc = acc + dot_nn(u_v[0, :, block(j)], wbuf[4 + j])
        h2 = (h1_v[0].astype(F32) + (acc + vec_ref[c, 5:6, :])).astype(BF)
        home = (leg == 1) & (pos == 0) & (i < OWN)
        inside = (leg == 0) & (pos == 3)
        buf[jnp.where(home, YO + i, jnp.where(inside, HV + MICRO + i, OUT + k))] = h2

        @pl.when(hops_out(FWD, leg))
        def _():
            hop(FWD, leg, i).start()

        @pl.when(home)
        def _():
            to_home(YO + i, i, y_hbm, send_y, recv_y.at[0], True)

        saves[5].start()
        saves[6].start()
        release(4, 5, 6, 7)

    def backward_task(leg, i, before_kind, before_leg, before_i, next_kind, next_leg, next_i, need, release):
        c = copy_of(leg)
        k = leg * MICRO + i
        loads, later = b_loads(leg, i), b_loads(next_leg, next_i)

        @pl.when(before_kind == FWD)
        def _():
            for ld in loads:
                ld.start()

        def prefetch(n):
            @pl.when(next_kind == BWD)
            def _():
                later[n].start()

        def both(ref_value):
            return ref_value.reshape(ROWS, ref_value.shape[-1])

        def pieces(v):
            return v.reshape(PAIR, SEQ, v.shape[-1])

        @pl.when((leg == 1) & (pos == 0))
        def _():
            for r in range(PAIR):
                pltpu.make_async_copy(dy_hbm, buf.at[DV + k + r], recv_dy.at[i + r]).wait()

        @pl.when(hops_in(BWD, leg))
        def _():
            hop(BWD, leg, i).wait_recv()

        saves = b_saves(leg, i)
        saves[3].start()
        need(4, 5, 6, 7)
        loads[0].wait()

        def tally(ref, row, cols, v):
            ref[c, row:row + 1, cols] += rounded(jnp.sum(v, axis=0, keepdims=True))

        def norm_back(row, before_norm, d_out):
            xh, rstd = normalize(before_norm.astype(F32))
            d_out = rounded(d_out)
            tally(gvec_ref, row, every, d_out * xh)
            tally(gvec_ref, row + 1, every, d_out)
            gx = d_out * vec_ref[c, row:row + 1, :]
            m1 = jnp.mean(gx, axis=-1, keepdims=True)
            m2 = jnp.mean(gx * xh, axis=-1, keepdims=True)
            return rounded(rstd * (gx - m1 - xh * m2))

        every = slice(0, DM)
        dh2 = both(buf[pl.ds(DV + k, PAIR)])

        def hidden(j):
            dz = rounded(dot_nt(dh2, wbuf[4 + j])) * both(z_v[:, :, block(j)])
            for r in range(PAIR):
                tally(gbf_ref, 0, block(j), dz[r * SEQ:(r + 1) * SEQ])
            u_v[:, :, block(j)] = pieces(dz.astype(BF))

        hidden(0)
        dn2 = jnp.zeros((ROWS, DM), F32)
        for j in range(4):
            if j < 3:
                hidden(j + 1)
            dn2 = dn2 + dot_nt(both(u_v[:, :, block(j)]), w1buf[leg, j])
        saves[0].start()
        release(4, 5, 6, 7)
        prefetch(0)
        need(3)
        loads[1].wait()
        for r in range(PAIR):
            dh2f = buf[DV + k + r].astype(F32)
            tally(gvec_ref, 5, every, dh2f)
            dh1_v[r] = (dh2f + norm_back(3, h1_v[r], dn2[r * SEQ:(r + 1) * SEQ])).astype(BF)
            tally(gvec_ref, 2, every, dh1_v[r].astype(F32))
        do_v[...] = pieces(dot_nt(both(dh1_v[...]), wbuf[3]).astype(BF))
        saves[2].start()
        release(3)
        prefetch(1)
        need(0, 1, 2)
        loads[2].wait()
        loads[3].wait()

        @pl.when(before_kind == BWD)
        def _():
            b_saves(before_leg, before_i)[1].wait()

        @pl.when(hops_out(FWD, leg))
        def _():
            for r in range(PAIR):
                hop(FWD, leg, i + r).wait_send()

        def scores_back(r):
            dos = [split_heads(d) for d in heads(do_v, r, 0)]
            dps = [dot_nt(d, v) for d, v in zip(dos, heads(t_v, r, 2))]
            dss = []
            for n, dpv in enumerate(dps):
                p, dpv = p_v[r, n], rounded(dpv)
                dss.append((p * (dpv - jnp.sum(dpv * p, axis=-1, keepdims=True)) * 0.125).astype(BF))
            return dos, dss

        def heads_back(r, dos, dss):
            for n, (q, kk) in enumerate(zip(heads(t_v, r, 0), heads(t_v, r, 1))):
                lo = n * SEQ
                dt_v[r, :, lo:lo + SEQ] = dot_nn(side_by_side(dss[n]), split_heads(kk)).astype(BF)
                dt_v[r, :, DM + lo:DM + lo + SEQ] = dot_tn(dss[n], split_heads(q)).astype(BF)
                dt_v[r, :, 2 * DM + lo:2 * DM + lo + SEQ] = dot_tn(p_v[r, n].astype(BF), dos[n]).astype(BF)

        def input_back(r):
            da = jnp.zeros((SEQ, DM), F32)
            for j in range(3):
                dtj = dt_v[r, :, block(j)]
                tally(gbq_ref, 0, block(j), dtj.astype(F32))
                da = da + dot_nn(dtj, wbuf[j])
            dh = dh1_v[r].astype(F32) + norm_back(0, buf[HV + k + r], da)
            buf[jnp.where((leg == 1) & (pos == 3), DV + i, OUT + k) + r] = dh.astype(BF)

        ahead = [scores_back(r) for r in range(PAIR)]
        for r in range(PAIR):
            heads_back(r, *ahead[r])
            input_back(r)

        @pl.when(hops_out(BWD, leg))
        def _():
            hop(BWD, leg, i).start()

        @pl.when((leg == 0) & (pos == 0))
        def _():
            for r in range(PAIR):
                to_home(OUT + i + r, i + r, dx_hbm, send_dx, recv_dx.at[0], True)

        saves[1].start()
        prefetch(2)
        prefetch(3)
        release(0, 1, 2)

    def slot(s, carry):
        kind, leg, i = parts(code_at(s))
        before_kind, before_leg, before_i = parts(code_at(jnp.maximum(s - 1, 0)))
        next_kind, next_leg, next_i = parts(code_at(jnp.minimum(s + 1, N_TASKS - 1)))
        next_kind = jnp.where(s == N_TASKS - 1, 2, next_kind)
        before_kind = jnp.where(s == 0, 2, before_kind)
        need, release = weights_for(leg, next_leg, (s == 0) | (before_leg != leg), next_leg != leg)

        @pl.when(before_kind == FWD)
        def _():
            for n, sv in enumerate(f_saves(before_leg, before_i)):
                if n not in (5, 6):
                    sv.wait()

        @pl.when(before_kind == BWD)
        def _():
            for n in (0, 2, 3):
                b_saves(before_leg, before_i)[n].wait()

        @pl.when(kind == FWD)
        def _():
            @pl.when(before_kind == BWD)
            def _():
                b_saves(before_leg, before_i)[1].wait()

            forward_task(leg, i, before_kind, before_leg, before_i, need, release)

        @pl.when(kind == BWD)
        def _():
            @pl.when(before_kind == FWD)
            def _():
                for sv in f_saves(before_leg, before_i)[5:7]:
                    sv.wait()

            backward_task(leg, i, before_kind, before_leg, before_i, next_kind, next_leg, next_i, need, release)

        return carry

    lax.fori_loop(0, N_TASKS, slot, 0)
    _, last_leg, last_i = parts(codes[N_TASKS - 1])
    for sv in b_saves(last_leg, last_i):
        sv.wait()

    def finish(n, carry):
        leg, i = n // PAIRS, (n % PAIRS) * PAIR

        @pl.when(hops_out(BWD, leg))
        def _():
            hop(BWD, leg, i).wait_send()

        return carry

    lax.fori_loop(0, 2 * PAIRS, finish, 0)

    @pl.when(pos == 0)
    def _():
        for i in range(OWN):
            to_home(YO + i, jnp.int32(i), y_hbm, send_y, recv_y.at[0], False)
            to_home(OUT + i, jnp.int32(i), dx_hbm, send_dx, recv_dx.at[0], False)

    for src, send in ((x_hbm, send_x), (dy_hbm, send_dy)):
        for n in range(2):
            @pl.when(me != 7 * n)
            def _():
                pltpu.make_async_remote_copy(src_ref=src, dst_ref=buf.at[HV], send_sem=send.at[n], recv_sem=recv_x.at[0],
                                             device_id=(dp, 7 * n), device_id_type=MESH).wait_send()
    pltpu.make_async_copy(buf.at[YO], y_hbm, recv_y.at[0]).wait()
    pltpu.make_async_copy(buf.at[YO], dx_hbm, recv_dx.at[0]).wait()


def run_chain(x, dy, wq, wo, w1, w2, bq, bf, vec):
    hbm = pl.BlockSpec(memory_space=pltpu.HBM)
    vmem = pl.BlockSpec(memory_space=pltpu.VMEM)
    dma = pltpu.SemaphoreType.DMA

    def saved(n, ty=BF):
        return jax.ShapeDtypeStruct((2, MICRO, SEQ, n), ty)

    def paired(n, ty=BF):
        return pltpu.VMEM((PAIR, SEQ, n), ty)

    single = pltpu.VMEM((SEQ, DM), BF)
    return pl.pallas_call(
        chain_kernel,
        out_shape=(
            jax.ShapeDtypeStruct((SEQ, DM), BF), jax.ShapeDtypeStruct((SEQ, DM), BF),
            saved(DM), saved(3 * DM), saved(DM), saved(DM), saved(DM), saved(FF, F32), saved(FF),
            jax.ShapeDtypeStruct((2, MICRO, 8, 2 * SEQ, SEQ), F32),
            saved(FF), saved(3 * DM), saved(DM), saved(DM),
            jax.ShapeDtypeStruct((2, 1, 3 * DM), F32), jax.ShapeDtypeStruct((2, 1, FF), F32), jax.ShapeDtypeStruct((2, 8, DM), F32),
        ),
        in_specs=[hbm] * 6 + [vmem] * 3,
        out_specs=tuple([hbm] * 14 + [vmem] * 3),
        scratch_shapes=[
            pltpu.VMEM((2, 1, 3 * DM), F32), pltpu.VMEM((2, 1, FF), F32), pltpu.VMEM((2, 8, DM), F32),
            pltpu.VMEM((8, DM, DM), BF),
            pltpu.VMEM((2, 4, DM, DM), BF),
            pltpu.VMEM((N_SLOTS, SEQ, DM), BF),
            single, paired(3 * DM), single, paired(DM), single, paired(FF, F32), paired(FF),
            pltpu.VMEM((PAIR, 8, 2 * SEQ, SEQ), F32), paired(3 * DM), paired(DM), paired(DM),
            dma((8,)), dma((8,)), dma((8,)), dma((4,)), dma((4,)), dma((MICRO,)), dma((MICRO,)), dma((2,)), dma((2,)),
            dma((2 * MICRO,)), dma((2 * MICRO,)), dma((2 * PAIRS,)), dma((2 * PAIRS,)),
            dma((OWN,)), dma((1,)), dma((OWN,)), dma((1,)),
        ],
        compiler_params=pltpu.CompilerParams(collective_id=0, has_side_effects=True, vmem_limit_bytes=67000000),
        name="chain",
    )(x, dy, wq, wo, w1, w2, bq, bf, vec)


N_TILES = 24
STRIP = 256


def wgrad_kernel(dt_hbm, a_hbm, o_hbm, dh1_hbm, n2_hbm, dz_hbm, u_hbm, dh2_hbm, y_in, dx_in, gbq_in, gbf_in, gvec_in,
                 gq_hbm, go_hbm, g1_hbm, g2_hbm, y_hbm, dx_hbm, gbq_ref, gbf_ref, gvec_ref, l_v, r_v, out_v, pass_v,
                 lsem, rsem, osem, psem):
    side = lax.axis_index('pp') // 4

    def tile(n, act):
        leg, b = n // 12, n % 12
        c = leg + side - 2 * leg * side
        at = n % 2

        def cols(j):
            return pl.ds(pl.multiple_of(j * DM, DM), DM)

        def three(left, right, out):
            if act == 'load':
                pltpu.make_async_copy(left, l_v.at[at], lsem.at[at]).start()
                pltpu.make_async_copy(right, r_v.at[at], rsem.at[at]).start()
            else:
                pltpu.make_async_copy(out_v.at[at], out, osem.at[at]).start()

        @pl.when(b < 3)
        def _():
            three(dt_hbm.at[leg, :, :, cols(b)], a_hbm.at[leg], gq_hbm.at[c, cols(b), :])

        @pl.when(b == 3)
        def _():
            three(o_hbm.at[leg], dh1_hbm.at[leg], go_hbm.at[c])

        @pl.when((b > 3) & (b < 8))
        def _():
            j = b - 4
            three(n2_hbm.at[leg], dz_hbm.at[leg, :, :, cols(j)], g1_hbm.at[c, :, cols(j)])

        @pl.when(b > 7)
        def _():
            j = b - 8
            three(u_hbm.at[leg, :, :, cols(j)], dh2_hbm.at[leg], g2_hbm.at[c, cols(j), :])

    tile(jnp.int32(0), 'load')

    def passing(act):
        for n, (src, dst) in enumerate(((y_in, y_hbm), (dx_in, dx_hbm))):
            into = pltpu.make_async_copy(src, pass_v.at[n], psem.at[n])
            out = pltpu.make_async_copy(pass_v.at[n], dst, psem.at[n])
            if act == 'in':
                into.start()
            elif act == 'out':
                into.wait()
                out.start()
            else:
                out.wait()

    passing('in')
    gbf_ref[...] = gbf_in[...]
    for c in range(2):
        for n in range(6):
            gvec_ref[c, n] = gvec_in[c, n:n + 1, :]
        for n in range(48):
            gbq_ref[c, n // 16, n % 16:n % 16 + 1, :] = gbq_in[c, :, n * 64:(n + 1) * 64]
    passing('out')

    def step(n, carry):
        at = n % 2

        @pl.when(n + 1 < N_TILES)
        def _():
            tile(n + 1, 'load')

        pltpu.make_async_copy(a_hbm.at[0], l_v.at[at], lsem.at[at]).wait()
        pltpu.make_async_copy(a_hbm.at[0], r_v.at[at], rsem.at[at]).wait()

        @pl.when(n > 1)
        def _():
            pltpu.make_async_copy(out_v.at[at], go_hbm.at[0], osem.at[at]).wait()

        for k in range(DM // STRIP):
            rows = slice(k * STRIP, (k + 1) * STRIP)
            acc = rounded(dot_nn(l_v[at, 0, :, rows].T, r_v[at, 0]))
            for m in range(1, MICRO):
                acc = acc + rounded(dot_nn(l_v[at, m, :, rows].T, r_v[at, m]))
            out_v[at, rows, :] = acc
        tile(n, 'store')
        return carry

    lax.fori_loop(0, N_TILES, step, 0)
    for at in range(2):
        pltpu.make_async_copy(out_v.at[at], go_hbm.at[0], osem.at[at]).wait()
    passing('done')


def weight_grads(*saved):
    hbm = pl.BlockSpec(memory_space=pltpu.HBM)
    vmem = pl.BlockSpec(memory_space=pltpu.VMEM)
    dma = pltpu.SemaphoreType.DMA
    return pl.pallas_call(
        wgrad_kernel,
        out_shape=tuple(jax.ShapeDtypeStruct((2,) + s, F32) for s in ((3 * DM, DM), (DM, DM), (DM, FF), (FF, DM)))
        + (jax.ShapeDtypeStruct((SEQ, DM), BF),) * 2
        + tuple(jax.ShapeDtypeStruct((2,) + s, F32) for s in ((3, 16, 64), (1, FF), (6, 1, DM))),
        in_specs=[hbm] * 10 + [vmem] * 3,
        out_specs=tuple([hbm] * 6 + [vmem] * 3),
        scratch_shapes=[
            pltpu.VMEM((2, MICRO, SEQ, DM), BF), pltpu.VMEM((2, MICRO, SEQ, DM), BF), pltpu.VMEM((2, DM, DM), F32),
            pltpu.VMEM((2, SEQ, DM), BF), dma((2,)), dma((2,)), dma((2,)), dma((2,)),
        ],
        compiler_params=pltpu.CompilerParams(vmem_limit_bytes=67000000),
        cost_estimate=pl.CostEstimate(flops=4 * MICRO * SEQ * 12 * DM * DM, bytes_accessed=N_TILES * 8 * DM * DM, transcendentals=0),
        name="wgrad",
    )(*saved)


def solution(mesh):
    data_spec = P(('dp', 'pp'))
    weight_spec = P('pp')

    def per_device(x_loc, dy_loc, w_qkv, w_attn, w_fc, w_proj, b_qkv, b_fc, vec_d):
        wq = jnp.transpose(w_qkv, (0, 1, 2, 4, 5, 6, 3)).reshape(2, 3 * DM, DM)
        bq = b_qkv.reshape(2, 3, 16, 64)
        bf = b_fc.reshape(2, FF)
        vec = jnp.transpose(vec_d.reshape(2, 6, DM), (1, 0, 2))
        (y, dx, a, _, o, _, n2, _, u, _, dz, dt, dh1, dh2, gbq, gbf, gvec) = run_chain(
            x_loc.reshape(SEQ, DM), dy_loc.reshape(SEQ, DM), wq, w_attn.reshape(2, DM, DM), w_fc.reshape(2, DM, FF),
            w_proj.reshape(2, FF, DM), bq, bf, vec)
        gq, go, g1, g2, y, dx, gbq, gbf, gvec = weight_grads(dt, a, o, dh1, n2, dz, u, dh2, y, dx, gbq, gbf, gvec)
        gq = jnp.transpose(gq.reshape(1, 2, 1, 3, 16, 64, DM), (0, 1, 2, 6, 3, 4, 5))
        return (
            y.reshape(x_loc.shape), dx.reshape(x_loc.shape), gq, go.reshape(w_attn.shape), g1.reshape(w_fc.shape),
            g2.reshape(w_proj.shape), gbq.reshape(b_qkv.shape), gbf.reshape(b_fc.shape), gvec.reshape(vec_d.shape),
        )

    return jax.shard_map(per_device, mesh=mesh, in_specs=(data_spec, data_spec) + (weight_spec,) * 7,
                         out_specs=(data_spec, data_spec) + (data_spec,) * 7, check_vma=False)
```

time: 4920 us -> 447 us (0.09)
  waiting for transfers between devices: 2130 us -> 0 us
  starting transfers between devices: 1080 us -> 0 us
  matrix products: 688 us -> 0 us
  other arithmetic: 463 us -> 0 us
  Pallas kernels: 0 us -> 446 us
  local copies, waits for them, and re-layouts: 402 us -> 0 us
  loops' own time: 129 us -> 0 us
    ppermute x58 -> x0, waiting for transfers between devices: 2130 us -> none  [the longest x7 1130 us: per_device(): peer_down = tuple((lax.ppermute(g, 'pp', opposite) for g in down_acc))]
    ppermute x58 -> x0, starting transfers between devices: 1080 us -> none  [the longest x11 719 us: backward_step(): up_cot_in = lax.ppermute(up_dx, 'pp', to_next)]
    dot_general x168 -> x0, matrix products: 662 us -> none  [the longest x24 184 us: gpt_layer(): jnp.dot(normed_two, w_fc, preferred_element_type=jnp.float32)]
    pallas_call x0 -> x2, Pallas kernels: none -> 446 us  [the longest x1 328 us: run_chain(): pl.pallas_call(chain_kernel, out_shape=(jax.ShapeDtypeStruct((SEQ, DM), B...]
    add x40 -> x0, other arithmetic: 147 us -> none  [stage_backward(): a + g.astype(jnp.float32)]
    convert_element_type x96 -> x0, local copies, waits for them, and re-layouts: 134 us -> none  [the longest x8 101 us: stage_backward(): g.astype(jnp.float32)]
    another operation x46 -> x0, loops' own time: 129 us -> none  [the longest x11 81.3 us: backward_step(): lax.cond(down_ok, stage_backward, skip_backward, pick_row(down_stash, dow...]
    another operation x14 -> x0, other arithmetic: 93.5 us -> none  [per_device(): jnp.stack([mine_d + peer_u, mine_u + peer_d], axis=0)[None]]
  transfers between devices with their start and end apart: 62 -> 0, of which waited for: 13 -> 0; matrix products, arithmetic and copies ran while one was open for 20% -> 0% of each run, Pallas kernels for 0% -> 0%
where the time goes in v1:
time: 447 us; the launch traced here: 446 us
  Pallas kernels  446 us (100%)
    pallas_call x1, Pallas kernels, run_chain(): pl.pallas_call(chain_kernel, out_shape=(jax.ShapeDtypeStruct((SEQ, DM), B...  328 us
    pallas_call x1, Pallas kernels, weight_grads(): pl.pallas_call(wgrad_kernel, out_shape=tuple((jax.ShapeDtypeStruct((2,) +...  117 us

profile of v1, /device:TPU:0, one launch (start us, length us, event | category | flops | bytes accessed | tf_op | source)
XLA Modules:
  0.0 446.5 jit_solution(2193773796282141925)
XLA Ops:
  0.6 328.2 %chain.1 = (bf16[128,1024]{1,0:T(8,128)(2,1)}, bf16[128,1024]{1,0:T(8,128)(2,1)}, bf16[2,8,128,1024]{3,2,1,0:T(8,128)(2,1)}, bf16[2,8,128,3072]{3,2,1,0:T(8,128)...) custom-call(bf16[128,1024]{1,0:T(8,128)(2,1)} %bitcast.40, ...), custom_call_target="tpu_custom_call" | custom-call | tf_op jit(solution)/shard_map/chain/pallas_call | solution.py:541
  328.9 117.4 %wgrad.1 = (f32[2,3072,1024]{2,1,0:T(8,128)}, f32[2,1024,1024]{2,1,0:T(8,128)}, f32[2,1024,4096]{2,1,0:T(8,128)}, f32[2,4096,1024]{2,1,0:T(8,128)}, bf16[128,102...) custom-call(bf16[2,8,128,3072]{3,2,1,0:T(8,128)(2,1)} %get-tuple-ele, ...), custom_call_target="tpu_custom_call" | custom-call | flops 51539607552 | bytes 201326592 | tf_op jit(solution)/shard_map/wgrad/pallas_call | solution.py:666

commit v2 on v1

v2 whole, which is shorter than its diff:
```python
import jax
import jax.numpy as jnp
from jax import lax
from jax.experimental import pallas as pl
from jax.experimental.pallas import tpu as pltpu
from jax.sharding import PartitionSpec as P

EPSILON = 1e-5
SEQ = 128
DM = 1024
FF = 4096
MICRO = 8
OWN = MICRO // 2
PAIR = 2
HV, DV, OUT, YO = 0, 2 * MICRO, 4 * MICRO, 4 * MICRO + 2 * OWN
D1 = YO + OWN
N_SLOTS = D1 + 2 * OWN
FWD, BWD, FWD_FAR, BWD_FAR, NONE = 0, 1, 2, 3, 4
N_TASKS = 24
ORDER = (
    (0x2da2ac6496080c1080, 0xdb44d2411fa693cb9b),
    (0x2d9298248983901080, 0xfb6d1349047cbac6da),
    (0xb982e42ac243201080, 0xfb4da64d24116daf19),
    (0x418bac2c3282241200, 0xfbcd369a44db49a459),
)
GELU_C = 0.7978845608028654
GELU_CA = GELU_C * 0.044715
NEG = -1e30
MESH = pl.DeviceIdType.MESH
BF = jnp.bfloat16
F32 = jnp.float32


def dot_nn(a, b):
    return lax.dot_general(a, b, (((1,), (0,)), ((), ())), preferred_element_type=F32)


def dot_nt(a, b):
    return lax.dot_general(a, b, (((1,), (1,)), ((), ())), preferred_element_type=F32)


def dot_tn(a, b):
    return lax.dot_general(a, b, (((0,), (0,)), ((), ())), preferred_element_type=F32)


def normalize(rows_f32):
    mean = jnp.mean(rows_f32, axis=-1, keepdims=True)
    centered = rows_f32 - mean
    var = jnp.mean(centered * centered, axis=-1, keepdims=True)
    rstd = lax.rsqrt(var + EPSILON)
    return centered * rstd, rstd


def rounded(v):
    return v.astype(BF).astype(F32)


def gelu_parts(z):
    zz = z * z
    th = jnp.tanh(z * (GELU_C + GELU_CA * zz))
    half = 0.5 + 0.5 * th
    return half, half + ((half * (1.0 - th)) * z) * (GELU_C + (3.0 * GELU_CA) * zz)


def block(j):
    return slice(j * DM, (j + 1) * DM)


def chain_kernel(x_hbm, dy_hbm, wq_hbm, wo_hbm, w1_hbm, w2_hbm, bq_in, bf_in, vec_in,
                 y_hbm, dx_hbm, a_hbm, t_hbm, o_hbm, h1_hbm, n2_hbm, z_hbm, u_hbm, p_hbm,
                 dz_hbm, dt_hbm, dh1_hbm, dh2_hbm, gbq_ref, gbf_ref, gvec_ref,
                 bq_ref, bf_ref, vec_ref, wbuf, w1buf, buf, a_v, t_v, o_v, h1_v, n2_v, z_v, u_v, p_v, dt_v, dh1_v, do_v, gln_v, gln_far,
                 wsem, w1sem, fsem, bsem, lsem, recv_x, recv_dy, send_x, send_dy,
                 send_f, recv_f, send_b, recv_b, send_fm, recv_fm, send_bm, recv_bm, send_d1, recv_d1, send_g, recv_g, send_y, recv_y, send_dx, recv_dx):
    me = lax.axis_index('pp')
    dp = lax.axis_index('dp')
    side = me // 4
    pos = me + side * (7 - 2 * me)

    def place(q):
        return (dp, q + side * (7 - 2 * q))

    def copy_of(leg):
        return leg + side - 2 * leg * side

    codes = []
    for s in range(N_TASKS):
        row = [jnp.int32((ORDER[q][s // 12] >> (6 * (s % 12))) % 64) for q in range(4)]
        codes.append(jnp.where(pos == 0, row[0], jnp.where(pos == 1, row[1], jnp.where(pos == 2, row[2], row[3]))))

    def code_at(s):
        c = codes[0]
        for k in range(1, N_TASKS):
            c = jnp.where(s == k, codes[k], c)
        return c

    def parts(code):
        return code // 16, (code // 8) % 2, code % 8

    barrier = pltpu.get_barrier_semaphore()
    for k in range(1, 8):
        pl.semaphore_signal(barrier, inc=1, device_id=(dp, lax.rem(me + k, 8)), device_id_type=MESH)

    def block_copy(b, leg):
        c = copy_of(leg)
        if b < 3:
            src = wq_hbm.at[c, pl.ds(b * DM, DM), :]
        elif b == 3:
            src = wo_hbm.at[c]
        else:
            src = w2_hbm.at[c, pl.ds((b - 4) * DM, DM), :]
        return pltpu.make_async_copy(src, wbuf.at[b], wsem.at[b])

    def w1_copy(j, leg):
        return pltpu.make_async_copy(w1_hbm.at[copy_of(leg), :, pl.ds(j * DM, DM)], w1buf.at[leg, j], w1sem.at[leg * 4 + j])

    first_leg = parts(codes[0])[1]
    for b in range(4):
        block_copy(b, first_leg).start()
    for j in range(4):
        w1_copy(j, first_leg).start()
        block_copy(4 + j, first_leg).start()
    for j in range(4):
        w1_copy(j, 1 - first_leg).start()

    for c in range(2):
        bf_ref[c] = bf_in[c:c + 1, :].astype(F32)
        for n in range(6):
            vec_ref[c, n:n + 1, :] = vec_in[n, c:c + 1, :].astype(F32)
        for n in range(24):
            pair = bq_in[c, n // 8, 2 * (n % 8):2 * (n % 8) + 2, :].astype(F32)
            bq_ref[c, :, n * SEQ:(n + 1) * SEQ] = jnp.concatenate([pair[:1], pair[1:]], axis=1)
    gbq_ref[...] = jnp.zeros_like(gbq_ref)
    gbf_ref[...] = jnp.zeros_like(gbf_ref)
    gln_v[...] = jnp.zeros_like(gln_v)

    pl.semaphore_wait(barrier, 7)

    def spread(src, base, send, recv):
        dst = buf.at[base + pos]

        @pl.when(pos == 0)
        def _():
            pltpu.make_async_copy(src, dst, recv.at[0]).start()

        @pl.when(pos != 0)
        def _():
            pltpu.make_async_remote_copy(src_ref=src, dst_ref=dst, send_sem=send.at[0], recv_sem=recv.at[pos],
                                         device_id=place(0), device_id_type=MESH).start()

    spread(x_hbm, HV, send_x, recv_x)
    spread(dy_hbm, DV + MICRO, send_dy, recv_dy)

    def upward(kind, leg):
        return leg if kind == BWD else 1 - leg

    def hop(kind, leg, i):
        k, n = leg * MICRO + i, leg * OWN + i
        q = pos - 1 + 2 * upward(kind, leg)
        base, send, recv = (HV, send_f, recv_f) if kind == FWD else (DV, send_b, recv_b)
        return pltpu.make_async_remote_copy(src_ref=buf.at[OUT + n], dst_ref=buf.at[base + k], send_sem=send.at[n],
                                            recv_sem=recv.at[n], device_id=place(q), device_id_type=MESH)

    def mirror(kind, leg, i):
        k, n = leg * MICRO + i, leg * OWN + i
        base, send, recv = (HV, send_fm, recv_fm) if kind == FWD else (DV, send_bm, recv_bm)
        return pltpu.make_async_remote_copy(src_ref=buf.at[base + k], dst_ref=buf.at[base + k + OWN], send_sem=send.at[n],
                                            recv_sem=recv.at[n], device_id=(dp, 7 - me), device_id_type=MESH)

    def mirror_dh1(leg, i):
        n = leg * OWN + i
        return pltpu.make_async_remote_copy(src_ref=dh1_v.at[0], dst_ref=buf.at[D1 + n], send_sem=send_d1.at[0],
                                            recv_sem=recv_d1.at[n], device_id=(dp, 7 - me), device_id_type=MESH)

    def mirror_sums():
        return pltpu.make_async_remote_copy(src_ref=gln_v, dst_ref=gln_far, send_sem=send_g.at[0], recv_sem=recv_g.at[0],
                                            device_id=(dp, 7 - me), device_id_type=MESH)

    def hops_out(kind, leg):
        up = upward(kind, leg)
        return ((up == 1) & (pos < 3)) | ((up == 0) & (pos > 0))

    def hops_in(kind, leg):
        up = upward(kind, leg)
        return ((up == 1) & (pos > 0)) | ((up == 0) & (pos < 3))

    def f_saves(leg, i, n):
        pairs = ((a_v, a_hbm), (t_v, t_hbm), (o_v, o_hbm), (h1_v, h1_hbm), (n2_v, n2_hbm), (z_v, z_hbm), (u_v, u_hbm), (p_v, p_hbm))
        return [pltpu.make_async_copy(v.at[pl.ds(0, n)], h.at[leg, pl.ds(i, n)], fsem.at[m]) for m, (v, h) in enumerate(pairs)]

    def flush_forward(kind, leg, i, which):
        for n, of_kind in ((1, FWD), (PAIR, FWD_FAR)):
            @pl.when(kind == of_kind)
            def _():
                saves = f_saves(leg, i, n)
                for m in which:
                    if n == 1 or m != 3:
                        saves[m].wait()

    def b_saves(leg, i, n):
        own = pl.ds(0, n)
        dh1 = dh1_v if n == 1 else buf.at[pl.ds(D1 + leg * OWN + i - OWN, n)]
        pairs = ((u_v.at[pl.ds(PAIR - n, n)], dz_hbm), (dt_v.at[own], dt_hbm), (dh1, dh1_hbm), (buf.at[pl.ds(DV + leg * MICRO + i, n)], dh2_hbm))
        return [pltpu.make_async_copy(v, h.at[leg, pl.ds(i, n)], bsem.at[m]) for m, (v, h) in enumerate(pairs)]

    def b_loads(leg, i, n):
        pairs = ((z_hbm, z_v), (h1_hbm, h1_v), (t_hbm, t_v), (p_hbm, p_v))
        return [pltpu.make_async_copy(h.at[leg, pl.ds(i, n)], v.at[pl.ds(0, n)], lsem.at[m]) for m, (h, v) in enumerate(pairs)]

    def flush_backward(kind, leg, i, which):
        for n, of_kind in ((1, BWD), (PAIR, BWD_FAR)):
            @pl.when(kind == of_kind)
            def _():
                saves = b_saves(leg, i, n)
                for m in which:
                    saves[m].wait()

    def to_home(slot, i, dst, send, recv, starting):
        src = buf.at[slot]

        @pl.when(i == 0)
        def _():
            if starting:
                pltpu.make_async_copy(src, dst, recv).start()

        @pl.when((i > 0) & (i < OWN))
        def _():
            rc = pltpu.make_async_remote_copy(src_ref=src, dst_ref=dst, send_sem=send.at[i], recv_sem=recv,
                                              device_id=place(i), device_id_type=MESH)
            if starting:
                rc.start()
            else:
                rc.wait_send()

    lane = lax.broadcasted_iota(jnp.int32, (1, SEQ), 1)
    low = jnp.where(lane < 64, 1.0, 0.0).astype(BF)
    high = jnp.where(lane < 64, 0.0, 1.0).astype(BF)
    q_idx = lax.broadcasted_iota(jnp.int32, (2 * SEQ, SEQ), 0) % SEQ
    k_idx = lax.broadcasted_iota(jnp.int32, (2 * SEQ, SEQ), 1)
    causal = q_idx >= k_idx

    def split_heads(v):
        return jnp.concatenate([v * low, v * high], axis=0)

    def side_by_side(v):
        return jnp.concatenate([v[:SEQ], v[SEQ:]], axis=1)

    def heads(ref, r, part):
        return [ref[r, :, part * DM + p * SEQ:part * DM + (p + 1) * SEQ] for p in range(8)]

    def probs(s):
        s = jnp.where(causal, s * 0.125, NEG)
        e = jnp.exp(s - jnp.max(s, axis=-1, keepdims=True))
        return e * (1.0 / jnp.sum(e, axis=-1, keepdims=True))

    def weights_for(leg, next_leg, fresh, moving):
        def need(*blocks):
            @pl.when(fresh)
            def _():
                for b in blocks:
                    block_copy(b, leg).wait()

        def release(*blocks):
            @pl.when(moving)
            def _():
                for b in blocks:
                    block_copy(b, next_leg).start()

        return need, release

    def flat(v):
        return v.reshape(v.shape[0] * v.shape[1], v.shape[2])

    def pieces(v):
        return v.reshape(v.shape[0] // SEQ, SEQ, v.shape[1])

    def forward_task(n, far, leg, i, before_kind, before_leg, before_i, need, release):
        c = copy_of(leg)
        k = leg * MICRO + i
        own = slice(0, n)

        if far:
            for r in range(n):
                mirror(FWD, leg, i - OWN + r).wait_recv()
        else:
            @pl.when((leg == 0) & (pos == 0))
            def _():
                pltpu.make_async_copy(x_hbm, buf.at[HV + i], recv_x.at[i]).wait()

            @pl.when(hops_in(FWD, leg))
            def _():
                hop(FWD, leg, i).wait_recv()

            mirror(FWD, leg, i).start()

        saves = f_saves(leg, i, n)
        need(0, 1, 2)
        xh, _ = normalize(flat(buf[pl.ds(HV + k, n)]).astype(F32))
        a_v[own] = pieces((xh * vec_ref[c, 0:1, :] + vec_ref[c, 1:2, :]).astype(BF))
        for j in range(3):
            t_v[own, :, block(j)] = pieces((dot_nt(flat(a_v[own]), wbuf[j]) + bq_ref[c, :, block(j)]).astype(BF))
        saves[0].start()
        saves[1].start()
        release(0, 1, 2)
        ss = [[dot_nt(split_heads(q), kk) for q, kk in zip(heads(t_v, r, 0), heads(t_v, r, 1))] for r in range(n)]
        ps = [[probs(sc) for sc in row] for row in ss]
        for r in range(n):
            for m, (p, v) in enumerate(zip(ps[r], heads(t_v, r, 2))):
                p_v[r, m] = p
                o_v[r, :, m * SEQ:(m + 1) * SEQ] = dot_nn(side_by_side(p.astype(BF)), split_heads(v)).astype(BF)
        saves[2].start()
        saves[7].start()
        need(3)
        h1 = flat(buf[pl.ds(HV + k, n)]).astype(F32) + dot_nn(flat(o_v[own]), wbuf[3]) + vec_ref[c, 2:3, :]
        h1_v[own] = pieces(h1.astype(BF))
        xh, _ = normalize(flat(h1_v[own]).astype(F32))
        n2_v[own] = pieces((xh * vec_ref[c, 3:4, :] + vec_ref[c, 4:5, :]).astype(BF))
        if not far:
            saves[3].start()
        saves[4].start()
        release(3)
        need(4, 5, 6, 7)

        @pl.when(i == 0)
        def _():
            for j in range(4):
                w1_copy(j, leg).wait()

        flush_forward(before_kind, before_leg, before_i, (5, 6))

        def hidden(j):
            z = dot_nn(flat(n2_v[own]), w1buf[leg, j]) + bf_ref[c, :, block(j)]
            half, slope = gelu_parts(z)
            u_v[own, :, block(j)] = pieces((z * half).astype(BF))
            z_v[own, :, block(j)] = pieces(z if far else slope)

        hidden(0)
        acc = jnp.zeros((n * SEQ, DM), F32)
        for j in range(4):
            if j < 3:
                hidden(j + 1)
            if not far:
                acc = acc + dot_nn(flat(u_v[own, :, block(j)]), wbuf[4 + j])
        if not far:
            h2 = (flat(h1_v[own]).astype(F32) + (acc + vec_ref[c, 5:6, :])).astype(BF)
            home = (leg == 1) & (pos == 0)
            inside = (leg == 0) & (pos == 3)
            buf[jnp.where(home, YO + i, jnp.where(inside, HV + MICRO + i, OUT + leg * OWN + i))] = h2

            @pl.when(hops_out(FWD, leg))
            def _():
                hop(FWD, leg, i).start()

            @pl.when(home)
            def _():
                to_home(YO + i, i, y_hbm, send_y, recv_y.at[0], True)

        saves[5].start()
        saves[6].start()
        release(4, 5, 6, 7)

    def backward_task(n, far, leg, i, before_kind, before_leg, before_i, next_kind, next_leg, next_i, need, release):
        c = copy_of(leg)
        k = leg * MICRO + i
        own, dz_at = slice(0, n), slice(PAIR - n, PAIR)
        loads = b_loads(leg, i, n)

        after_b = (before_kind == BWD) | (before_kind == BWD_FAR)

        inplace = (before_kind == FWD) & (before_leg == leg) & (before_i == i) & (not far)

        @pl.when(jnp.logical_not(inplace))
        def _():
            flush_forward(before_kind, before_leg, before_i, (5, 6))

        @pl.when(jnp.logical_not(after_b | inplace))
        def _():
            for m, ld in enumerate(loads):
                if m != 1 or not far:
                    ld.start()

        def arrived(*which):
            @pl.when(jnp.logical_not(inplace))
            def _():
                for m in which:
                    loads[m].wait()

        def prefetch(m):
            for next_n, of_kind in ((1, BWD), (PAIR, BWD_FAR)):
                if m != 1 or of_kind == BWD:
                    @pl.when(next_kind == of_kind)
                    def _():
                        b_loads(next_leg, next_i, next_n)[m].start()

        if far:
            for r in range(n):
                mirror(BWD, leg, i - OWN + r).wait_recv()
        else:
            @pl.when((leg == 1) & (pos == 0))
            def _():
                pltpu.make_async_copy(dy_hbm, buf.at[DV + k], recv_dy.at[i]).wait()

            @pl.when(hops_in(BWD, leg))
            def _():
                hop(BWD, leg, i).wait_recv()

            mirror(BWD, leg, i).start()

        def tally(ref, at, row, cols, v):
            ref[at, row:row + 1, cols] += rounded(jnp.sum(v, axis=0, keepdims=True))

        saves = b_saves(leg, i, n)
        saves[3].start()
        need(4, 5, 6, 7)
        if far:
            arrived(0)
        else:
            arrived(0, 1)
            second_norm = normalize(h1_v[0].astype(F32))
            first_norm = normalize(buf[HV + k].astype(F32))
            tally(gln_v, leg, 5, slice(0, DM), buf[DV + k].astype(F32))

        def norm_back(row, normalized, d_out):
            xh, rstd = normalized
            d_out = rounded(d_out)
            tally(gln_v, leg, row, every, d_out * xh)
            tally(gln_v, leg, row + 1, every, d_out)
            gx = d_out * vec_ref[c, row:row + 1, :]
            m1 = jnp.mean(gx, axis=-1, keepdims=True)
            m2 = jnp.mean(gx * xh, axis=-1, keepdims=True)
            return rounded(rstd * (gx - m1 - xh * m2))

        every = slice(0, DM)
        dh2 = flat(buf[pl.ds(DV + k, n)])

        def hidden(j):
            z = flat(z_v[own, :, block(j)])
            dz = rounded(dot_nt(dh2, wbuf[4 + j])) * (gelu_parts(z)[1] if far else z)
            for r in range(n):
                tally(gbf_ref, c, 0, block(j), dz[r * SEQ:(r + 1) * SEQ])
            u_v[dz_at, :, block(j)] = pieces(dz.astype(BF))

        hidden(0)
        dn2 = jnp.zeros((n * SEQ, DM), F32)
        for j in range(4):
            if j < 3:
                hidden(j + 1)
            if not far:
                dn2 = dn2 + dot_nt(flat(u_v[dz_at, :, block(j)]), w1buf[leg, j])
        saves[0].start()
        release(4, 5, 6, 7)
        prefetch(0)
        need(3)
        if far:
            for r in range(n):
                mirror_dh1(leg, i - OWN + r).wait_recv()
            dh1 = flat(buf[pl.ds(D1 + leg * OWN + i - OWN, n)])
        else:
            @pl.when((leg == 0) | (i > 0))
            def _():
                mirror_dh1(leg, i).wait_send()

            dh1_v[0] = (buf[DV + k].astype(F32) + norm_back(3, second_norm, dn2)).astype(BF)
            mirror_dh1(leg, i).start()
            dh1 = dh1_v[0]
            tally(gln_v, leg, 2, every, dh1.astype(F32))
        do_v[own] = pieces(dot_nt(dh1, wbuf[3]).astype(BF))
        saves[2].start()
        release(3)
        prefetch(1)
        need(0, 1, 2)
        arrived(2, 3)

        @pl.when(inplace)
        def _():
            flush_forward(before_kind, before_leg, before_i, (5, 6))

        flush_backward(before_kind, before_leg, before_i, (1,))
        if not far:
            @pl.when(hops_out(FWD, leg))
            def _():
                hop(FWD, leg, i).wait_send()

        def scores_back(r):
            dos = [split_heads(d) for d in heads(do_v, r, 0)]
            dps = [dot_nt(d, v) for d, v in zip(dos, heads(t_v, r, 2))]
            dss = []
            for m, dpv in enumerate(dps):
                p, dpv = p_v[r, m], rounded(dpv)
                dss.append((p * (dpv - jnp.sum(dpv * p, axis=-1, keepdims=True)) * 0.125).astype(BF))
            return dos, dss

        def heads_back(r, dos, dss):
            for m, (q, kk) in enumerate(zip(heads(t_v, r, 0), heads(t_v, r, 1))):
                lo = m * SEQ
                dt_v[r, :, lo:lo + SEQ] = dot_nn(side_by_side(dss[m]), split_heads(kk)).astype(BF)
                dt_v[r, :, DM + lo:DM + lo + SEQ] = dot_tn(dss[m], split_heads(q)).astype(BF)
                dt_v[r, :, 2 * DM + lo:2 * DM + lo + SEQ] = dot_tn(p_v[r, m].astype(BF), dos[m]).astype(BF)

        def input_back(r):
            da = jnp.zeros((SEQ, DM), F32)
            for j in range(3):
                dtj = dt_v[r, :, block(j)]
                tally(gbq_ref, c, 0, block(j), dtj.astype(F32))
                if not far:
                    da = da + dot_nn(dtj, wbuf[j])
            if not far:
                dh = dh1_v[r].astype(F32) + norm_back(0, first_norm, da)
                buf[jnp.where((leg == 1) & (pos == 3), DV + i, OUT + leg * OWN + i) + r] = dh.astype(BF)

        ahead = [scores_back(r) for r in range(n)]
        for r in range(n):
            heads_back(r, *ahead[r])
            input_back(r)

        if not far:
            @pl.when(hops_out(BWD, leg))
            def _():
                hop(BWD, leg, i).start()

            @pl.when((leg == 0) & (pos == 0))
            def _():
                to_home(OUT + i, i, dx_hbm, send_dx, recv_dx.at[0], True)

            @pl.when((leg == 0) & (i == OWN - 1))
            def _():
                mirror_sums().start()

        saves[1].start()
        prefetch(2)
        prefetch(3)
        release(0, 1, 2)

    def slot(s, carry):
        kind, leg, i = parts(code_at(s))
        before_kind, before_leg, before_i = parts(code_at(jnp.maximum(s - 1, 0)))
        next_kind, next_leg, next_i = parts(code_at(jnp.minimum(s + 1, N_TASKS - 1)))
        next_kind = jnp.where(s == N_TASKS - 1, NONE, next_kind)
        before_kind = jnp.where(s == 0, NONE, before_kind)
        need, release = weights_for(leg, next_leg, (s == 0) | (before_leg != leg), next_leg != leg)
        flush_forward(before_kind, before_leg, before_i, (0, 1, 2, 3, 4, 7))

        flush_backward(before_kind, before_leg, before_i, (0, 2, 3))
        for n, of_kind in ((1, FWD), (PAIR, FWD_FAR)):
            @pl.when(kind == of_kind)
            def _():
                flush_backward(before_kind, before_leg, before_i, (1,))
                forward_task(n, of_kind == FWD_FAR, leg, i, before_kind, before_leg, before_i, need, release)

        for n, of_kind in ((1, BWD), (PAIR, BWD_FAR)):
            @pl.when(kind == of_kind)
            def _():
                backward_task(n, of_kind == BWD_FAR, leg, i, before_kind, before_leg, before_i, next_kind, next_leg, next_i, need, release)

        return carry

    lax.fori_loop(0, N_TASKS, slot, 0)
    flush_backward(*parts(codes[N_TASKS - 1]), (0, 1, 2, 3))
    for leg in range(2):
        for i in range(OWN):
            mirror(FWD, leg, i).wait_send()
            mirror(BWD, leg, i).wait_send()

            @pl.when(hops_out(BWD, leg))
            def _():
                hop(BWD, leg, i).wait_send()

    @pl.when(pos == 0)
    def _():
        for i in range(OWN):
            to_home(YO + i, jnp.int32(i), y_hbm, send_y, recv_y.at[0], False)
            to_home(OUT + i, jnp.int32(i), dx_hbm, send_dx, recv_dx.at[0], False)

    @pl.when(pos != 0)
    def _():
        for src, send in ((x_hbm, send_x), (dy_hbm, send_dy)):
            pltpu.make_async_remote_copy(src_ref=src, dst_ref=buf.at[HV], send_sem=send.at[0], recv_sem=recv_x.at[0],
                                         device_id=place(0), device_id_type=MESH).wait_send()

    mirror_dh1(0, OWN - 1).wait_send()
    mirror_sums().wait()
    for leg in range(2):
        gvec_ref[copy_of(leg)] = gln_v[leg] + gln_far[leg]
    pltpu.make_async_copy(buf.at[YO], y_hbm, recv_y.at[0]).wait()
    pltpu.make_async_copy(buf.at[YO], dx_hbm, recv_dx.at[0]).wait()


def run_chain(x, dy, wq, wo, w1, w2, bq, bf, vec):
    hbm = pl.BlockSpec(memory_space=pltpu.HBM)
    vmem = pl.BlockSpec(memory_space=pltpu.VMEM)
    dma = pltpu.SemaphoreType.DMA

    def saved(n, ty=BF):
        return jax.ShapeDtypeStruct((2, MICRO, SEQ, n), ty)

    def paired(n, ty=BF):
        return pltpu.VMEM((PAIR, SEQ, n), ty)

    return pl.pallas_call(
        chain_kernel,
        out_shape=(
            jax.ShapeDtypeStruct((SEQ, DM), BF), jax.ShapeDtypeStruct((SEQ, DM), BF),
            saved(DM), saved(3 * DM), saved(DM), saved(DM), saved(DM), saved(FF, F32), saved(FF),
            jax.ShapeDtypeStruct((2, MICRO, 8, 2 * SEQ, SEQ), F32),
            saved(FF), saved(3 * DM), saved(DM), saved(DM),
            jax.ShapeDtypeStruct((2, 1, 3 * DM), F32), jax.ShapeDtypeStruct((2, 1, FF), F32), jax.ShapeDtypeStruct((2, 8, DM), F32),
        ),
        in_specs=[hbm] * 6 + [vmem] * 3,
        out_specs=tuple([hbm] * 14 + [vmem] * 3),
        scratch_shapes=[
            pltpu.VMEM((2, 1, 3 * DM), F32), pltpu.VMEM((2, 1, FF), F32), pltpu.VMEM((2, 8, DM), F32),
            pltpu.VMEM((8, DM, DM), BF),
            pltpu.VMEM((2, 4, DM, DM), BF),
            pltpu.VMEM((N_SLOTS, SEQ, DM), BF),
            paired(DM), paired(3 * DM), paired(DM), paired(DM), paired(DM), paired(FF, F32), paired(FF),
            pltpu.VMEM((PAIR, 8, 2 * SEQ, SEQ), F32), paired(3 * DM), pltpu.VMEM((1, SEQ, DM), BF), paired(DM),
            pltpu.VMEM((2, 8, DM), F32), pltpu.VMEM((2, 8, DM), F32),
            dma((8,)), dma((8,)), dma((8,)), dma((4,)), dma((4,)), dma((OWN,)), dma((OWN,)), dma((1,)), dma((1,)),
            *[dma((2 * OWN,))] * 8, dma((1,)), dma((2 * OWN,)), dma((1,)), dma((1,)),
            dma((OWN,)), dma((1,)), dma((OWN,)), dma((1,)),
        ],
        compiler_params=pltpu.CompilerParams(collective_id=0, has_side_effects=True, vmem_limit_bytes=67000000),
        name="chain",
    )(x, dy, wq, wo, w1, w2, bq, bf, vec)


N_TILES = 24
STRIP = 256


def wgrad_kernel(dt_hbm, a_hbm, o_hbm, dh1_hbm, n2_hbm, dz_hbm, u_hbm, dh2_hbm, y_in, dx_in, gbq_in, gbf_in, gvec_in,
                 gq_hbm, go_hbm, g1_hbm, g2_hbm, y_hbm, dx_hbm, gbq_ref, gbf_ref, gvec_ref, l_v, r_v, out_v, pass_v,
                 lsem, rsem, osem, psem):
    side = lax.axis_index('pp') // 4

    def tile(n, act):
        leg, b = n // 12, n % 12
        c = leg + side - 2 * leg * side
        at = n % 2

        def cols(j):
            return pl.ds(pl.multiple_of(j * DM, DM), DM)

        def three(left, right, out):
            if act == 'load':
                pltpu.make_async_copy(left, l_v.at[at], lsem.at[at]).start()
                pltpu.make_async_copy(right, r_v.at[at], rsem.at[at]).start()
            else:
                pltpu.make_async_copy(out_v.at[at], out, osem.at[at]).start()

        @pl.when(b < 3)
        def _():
            three(dt_hbm.at[leg, :, :, cols(b)], a_hbm.at[leg], gq_hbm.at[c, cols(b), :])

        @pl.when(b == 3)
        def _():
            three(o_hbm.at[leg], dh1_hbm.at[leg], go_hbm.at[c])

        @pl.when((b > 3) & (b < 8))
        def _():
            j = b - 4
            three(n2_hbm.at[leg], dz_hbm.at[leg, :, :, cols(j)], g1_hbm.at[c, :, cols(j)])

        @pl.when(b > 7)
        def _():
            j = b - 8
            three(u_hbm.at[leg, :, :, cols(j)], dh2_hbm.at[leg], g2_hbm.at[c, cols(j), :])

    tile(jnp.int32(0), 'load')

    def passing(act):
        for n, (src, dst) in enumerate(((y_in, y_hbm), (dx_in, dx_hbm))):
            into = pltpu.make_async_copy(src, pass_v.at[n], psem.at[n])
            out = pltpu.make_async_copy(pass_v.at[n], dst, psem.at[n])
            if act == 'in':
                into.start()
            elif act == 'out':
                into.wait()
                out.start()
            else:
                out.wait()

    passing('in')
    gbf_ref[...] = gbf_in[...]
    for c in range(2):
        for n in range(6):
            gvec_ref[c, n] = gvec_in[c, n:n + 1, :]
        for n in range(48):
            gbq_ref[c, n // 16, n % 16:n % 16 + 1, :] = gbq_in[c, :, n * 64:(n + 1) * 64]
    passing('out')

    def step(n, carry):
        at = n % 2

        @pl.when(n + 1 < N_TILES)
        def _():
            tile(n + 1, 'load')

        pltpu.make_async_copy(a_hbm.at[0], l_v.at[at], lsem.at[at]).wait()
        pltpu.make_async_copy(a_hbm.at[0], r_v.at[at], rsem.at[at]).wait()

        @pl.when(n > 1)
        def _():
            pltpu.make_async_copy(out_v.at[at], go_hbm.at[0], osem.at[at]).wait()

        for k in range(DM // STRIP):
            rows = slice(k * STRIP, (k + 1) * STRIP)
            acc = rounded(dot_nn(l_v[at, 0, :, rows].T, r_v[at, 0]))
            for m in range(1, MICRO):
                acc = acc + rounded(dot_nn(l_v[at, m, :, rows].T, r_v[at, m]))
            out_v[at, rows, :] = acc
        tile(n, 'store')
        return carry

    lax.fori_loop(0, N_TILES, step, 0)
    for at in range(2):
        pltpu.make_async_copy(out_v.at[at], go_hbm.at[0], osem.at[at]).wait()
    passing('done')


def weight_grads(*saved):
    hbm = pl.BlockSpec(memory_space=pltpu.HBM)
    vmem = pl.BlockSpec(memory_space=pltpu.VMEM)
    dma = pltpu.SemaphoreType.DMA
    return pl.pallas_call(
        wgrad_kernel,
        out_shape=tuple(jax.ShapeDtypeStruct((2,) + s, F32) for s in ((3 * DM, DM), (DM, DM), (DM, FF), (FF, DM)))
        + (jax.ShapeDtypeStruct((SEQ, DM), BF),) * 2
        + tuple(jax.ShapeDtypeStruct((2,) + s, F32) for s in ((3, 16, 64), (1, FF), (6, 1, DM))),
        in_specs=[hbm] * 10 + [vmem] * 3,
        out_specs=tuple([hbm] * 6 + [vmem] * 3),
        scratch_shapes=[
            pltpu.VMEM((2, MICRO, SEQ, DM), BF), pltpu.VMEM((2, MICRO, SEQ, DM), BF), pltpu.VMEM((2, DM, DM), F32),
            pltpu.VMEM((2, SEQ, DM), BF), dma((2,)), dma((2,)), dma((2,)), dma((2,)),
        ],
        compiler_params=pltpu.CompilerParams(vmem_limit_bytes=67000000),
        name="wgrad",
    )(*saved)


def solution(mesh):
    data_spec = P(('dp', 'pp'))
    weight_spec = P('pp')

    def per_device(x_loc, dy_loc, w_qkv, w_attn, w_fc, w_proj, b_qkv, b_fc, vec_d):
        wq = jnp.transpose(w_qkv, (0, 1, 2, 4, 5, 6, 3)).reshape(2, 3 * DM, DM)
        bq = b_qkv.reshape(2, 3, 16, 64)
        bf = b_fc.reshape(2, FF)
        vec = jnp.transpose(vec_d.reshape(2, 6, DM), (1, 0, 2))
        (y, dx, a, _, o, _, n2, _, u, _, dz, dt, dh1, dh2, gbq, gbf, gvec) = run_chain(
            x_loc.reshape(SEQ, DM), dy_loc.reshape(SEQ, DM), wq, w_attn.reshape(2, DM, DM), w_fc.reshape(2, DM, FF),
            w_proj.reshape(2, FF, DM), bq, bf, vec)
        gq, go, g1, g2, y, dx, gbq, gbf, gvec = weight_grads(dt, a, o, dh1, n2, dz, u, dh2, y, dx, gbq, gbf, gvec)
        gq = jnp.transpose(gq.reshape(1, 2, 1, 3, 16, 64, DM), (0, 1, 2, 6, 3, 4, 5))
        return (
            y.reshape(x_loc.shape), dx.reshape(x_loc.shape), gq, go.reshape(w_attn.shape), g1.reshape(w_fc.shape),
            g2.reshape(w_proj.shape), gbq.reshape(b_qkv.shape), gbf.reshape(b_fc.shape), gvec.reshape(vec_d.shape),
        )

    return jax.shard_map(per_device, mesh=mesh, in_specs=(data_spec, data_spec) + (weight_spec,) * 7,
                         out_specs=(data_spec, data_spec) + (data_spec,) * 7, check_vma=False)
```

time: 447 us -> 399 us (0.89)
  Pallas kernels: 446 us -> 398 us
    pallas_call x1, Pallas kernels: 328 us -> 281 us  [run_chain(): pl.pallas_call(chain_kernel, out_shape=(jax.ShapeDtypeStruct((SEQ, DM), B...]
where the time goes in v2:
time: 399 us
  Pallas kernels  398 us (100%)
    pallas_call x1, Pallas kernels, run_chain(): pl.pallas_call(chain_kernel, out_shape=(jax.ShapeDtypeStruct((SEQ, DM), B...  281 us
    pallas_call x1, Pallas kernels, weight_grads(): pl.pallas_call(wgrad_kernel, out_shape=tuple((jax.ShapeDtypeStruct((2,) +...  117 us

profile of v2, /device:TPU:0, one launch (start us, length us, event | category | flops | bytes accessed | tf_op | source)
XLA Modules:
  0.0 398.8 jit_solution(12310471778812321604)
XLA Ops:
  0.6 280.6 %chain.1 = (bf16[128,1024]{1,0:T(8,128)(2,1)}, bf16[128,1024]{1,0:T(8,128)(2,1)}, bf16[2,8,128,1024]{3,2,1,0:T(8,128)(2,1)}, bf16[2,8,128,3072]{3,2,1,0:T(8,128)...) custom-call(bf16[128,1024]{1,0:T(8,128)(2,1)} %bitcast.40, ...), custom_call_target="tpu_custom_call" | custom-call | tf_op jit(solution)/shard_map/chain/pallas_call | solution.py:599
  281.3 117.4 %wgrad.1 = (f32[2,3072,1024]{2,1,0:T(8,128)}, f32[2,1024,1024]{2,1,0:T(8,128)}, f32[2,1024,4096]{2,1,0:T(8,128)}, f32[2,4096,1024]{2,1,0:T(8,128)}, bf16[128,102...) custom-call(bf16[2,8,128,3072]{3,2,1,0:T(8,128)(2,1)} %get-tuple-ele, ...), custom_call_target="tpu_custom_call" | custom-call | tf_op jit(solution)/shard_map/wgrad/pallas_call | solution.py:725

commit v3 on v2

--- a/solution.py
+++ b/solution.py
@@ -12,16 +12,17 @@
 MICRO = 8
 OWN = MICRO // 2
 PAIR = 2
+WIDE = 256
 HV, DV, OUT, YO = 0, 2 * MICRO, 4 * MICRO, 4 * MICRO + 2 * OWN
 D1 = YO + OWN
 N_SLOTS = D1 + 2 * OWN
 FWD, BWD, FWD_FAR, BWD_FAR, NONE = 0, 1, 2, 3, 4
 N_TASKS = 24
 ORDER = (
-    (0x2da2ac6496080c1080, 0xdb44d2411fa693cb9b),
-    (0x2d9298248983901080, 0xfb6d1349047cbac6da),
-    (0xb982e42ac243201080, 0xfb4da64d24116daf19),
-    (0x418bac2c3282241200, 0xfbcd369a44db49a459),
+    (0x2da2992582240c2040, 0xd93d12450fbcb26b9b),
+    (0x2d9298266203902040, 0xdbe4f449143cb9bb1a),
+    (0xb982ec2a4243202040, 0xfb6993d1245b41af19),
+    (0x62eb242c3282241200, 0xf3eda6d136d2691650),
 )
 GELU_C = 0.7978845608028654
 GELU_CA = GELU_C * 0.044715
@@ -60,6 +61,15 @@
     th = jnp.tanh(z * (GELU_C + GELU_CA * zz))
     half = 0.5 + 0.5 * th
     return half, half + ((half * (1.0 - th)) * z) * (GELU_C + (3.0 * GELU_CA) * zz)
+
+
+def strip(j):
+    return slice(j * WIDE, (j + 1) * WIDE)
+
+
+def inside_block(j):
+    per = DM // WIDE
+    return j // per, slice(j % per * WIDE, (j % per + 1) * WIDE)
 
 
 def block(j):
@@ -215,19 +225,19 @@
                 for m in which:
                     saves[m].wait()
 
-    def to_home(slot, i, dst, send, recv, starting):
+    def to_home(slot, i, dst, send, recv, act):
         src = buf.at[slot]
 
         @pl.when(i == 0)
         def _():
-            if starting:
+            if act == 'start':
                 pltpu.make_async_copy(src, dst, recv).start()
 
         @pl.when((i > 0) & (i < OWN))
         def _():
             rc = pltpu.make_async_remote_copy(src_ref=src, dst_ref=dst, send_sem=send.at[i], recv_sem=recv,
                                               device_id=place(i), device_id_type=MESH)
-            if starting:
+            if act == 'start':
                 rc.start()
             else:
                 rc.wait_send()
@@ -329,18 +339,20 @@
         flush_forward(before_kind, before_leg, before_i, (5, 6))
 
         def hidden(j):
-            z = dot_nn(flat(n2_v[own]), w1buf[leg, j]) + bf_ref[c, :, block(j)]
+            b, cols = inside_block(j)
+            z = dot_nn(flat(n2_v[own]), w1buf[leg, b, :, cols]) + bf_ref[c, :, strip(j)]
             half, slope = gelu_parts(z)
-            u_v[own, :, block(j)] = pieces((z * half).astype(BF))
-            z_v[own, :, block(j)] = pieces(z if far else slope)
+            u_v[own, :, strip(j)] = pieces((z * half).astype(BF))
+            z_v[own, :, strip(j)] = pieces(z if far else slope)
 
         hidden(0)
         acc = jnp.zeros((n * SEQ, DM), F32)
-        for j in range(4):
-            if j < 3:
+        for j in range(FF // WIDE):
+            if j < FF // WIDE - 1:
                 hidden(j + 1)
             if not far:
-                acc = acc + dot_nn(flat(u_v[own, :, block(j)]), wbuf[4 + j])
+                b, rows = inside_block(j)
+                acc = acc + dot_nn(flat(u_v[own, :, strip(j)]), wbuf[4 + b, rows, :])
         if not far:
             h2 = (flat(h1_v[own]).astype(F32) + (acc + vec_ref[c, 5:6, :])).astype(BF)
             home = (leg == 1) & (pos == 0)
@@ -353,7 +365,7 @@
 
             @pl.when(home)
             def _():
-                to_home(YO + i, i, y_hbm, send_y, recv_y.at[0], True)
+                to_home(YO + i, i, y_hbm, send_y, recv_y.at[0], 'start')
 
         saves[5].start()
         saves[6].start()
@@ -520,7 +532,7 @@
 
             @pl.when((leg == 0) & (pos == 0))
             def _():
-                to_home(OUT + i, i, dx_hbm, send_dx, recv_dx.at[0], True)
+                to_home(OUT + i, i, dx_hbm, send_dx, recv_dx.at[0], 'start')
 
             @pl.when((leg == 0) & (i == OWN - 1))
             def _():
@@ -568,8 +580,8 @@
     @pl.when(pos == 0)
     def _():
         for i in range(OWN):
-            to_home(YO + i, jnp.int32(i), y_hbm, send_y, recv_y.at[0], False)
-            to_home(OUT + i, jnp.int32(i), dx_hbm, send_dx, recv_dx.at[0], False)
+            to_home(YO + i, jnp.int32(i), y_hbm, send_y, recv_y.at[0], 'wait')
+            to_home(OUT + i, jnp.int32(i), dx_hbm, send_dx, recv_dx.at[0], 'wait')
 
     @pl.when(pos != 0)
     def _():

time: 399 us -> 402 us (level)
  no operation moved by 1% of the time
where the time goes in v3:
time: 402 us
  Pallas kernels  401 us (100%)
    pallas_call x1, Pallas kernels, run_chain(): pl.pallas_call(chain_kernel, out_shape=(jax.ShapeDtypeStruct((SEQ, DM), B...  283 us
    pallas_call x1, Pallas kernels, weight_grads(): pl.pallas_call(wgrad_kernel, out_shape=tuple((jax.ShapeDtypeStruct((2,) +...  117 us

profile of v3, /device:TPU:0, one launch (start us, length us, event | category | flops | bytes accessed | tf_op | source)
XLA Modules:
  0.0 401.5 jit_solution(4076369296263202830)
XLA Ops:
  0.6 283.3 %chain.1 = (bf16[128,1024]{1,0:T(8,128)(2,1)}, bf16[128,1024]{1,0:T(8,128)(2,1)}, bf16[2,8,128,1024]{3,2,1,0:T(8,128)(2,1)}, bf16[2,8,128,3072]{3,2,1,0:T(8,128)...) custom-call(bf16[128,1024]{1,0:T(8,128)(2,1)} %bitcast.40, ...), custom_call_target="tpu_custom_call" | custom-call | tf_op jit(solution)/shard_map/chain/pallas_call | solution.py:611
  283.9 117.4 %wgrad.1 = (f32[2,3072,1024]{2,1,0:T(8,128)}, f32[2,1024,1024]{2,1,0:T(8,128)}, f32[2,1024,4096]{2,1,0:T(8,128)}, f32[2,4096,1024]{2,1,0:T(8,128)}, bf16[128,102...) custom-call(bf16[2,8,128,3072]{3,2,1,0:T(8,128)(2,1)} %get-tuple-ele, ...), custom_call_target="tpu_custom_call" | custom-call | tf_op jit(solution)/shard_map/wgrad/pallas_call | solution.py:737
